TPU v7x, 32 devices: a whole 2x2x4 slice. The times are simulated.
32 devices in a mesh: seq: 8 (over z, y), head: 4 (over x, core).
Axes of the slice: x: 2, y: 2, z: 4, core: 2. Of those that a mesh axis runs over, the one named last changes fastest.
Arguments:
- residual: bfloat16 [4096, 3072], P('seq', 'head'), may hold values from -6 to 6
- q_self: bfloat16 [4096, 3072], P('seq', 'head'), may hold values from -6 to 6
- k_self: bfloat16 [4096, 3072], P('seq', 'head'), may hold values from -6 to 6
- v_self: bfloat16 [4096, 3072], P('seq', 'head'), may hold values from -6 to 6
- w_out: bfloat16 [3072, 3072], P('head'), may hold values from -0.109375 to 0.109375
- norm_gain: float32 [3072], replicated, may hold values from 0.5 to 1.5
- w_query: bfloat16 [3072, 3072], P('seq', 'head')
- w_cache: bfloat16 [3072, 2048], P('seq', 'head')
- block_doc: int32 [8], replicated, may hold values from 0 to 2, never falling along the last dimension, each value on 1 to 4 neighbouring positions
- tail_len: int32 [8], replicated, may hold values from 1 to 512
Outputs:
- hidden: bfloat16 [4096, 3072], P('seq', 'head')
- cross_context: bfloat16 [4096, 3072], P('seq', 'head')
Inputs may be any that keep to these rules, and one draw needn't show every extreme that they name: block_doc never falls along the blocks; each document covers 1 to 4 consecutive blocks, and some document covers exactly 4. `tail_len`: read only for the last block of a document.
All inputs are finite; a program needn't handle non-finite values.
Results may differ from a plain program's by a relative error of at most 0.0078.
Values may be sent and summed in bfloat16 or wider, within the bound.
No kernel may reach another device: no remote copies, remote signals or barrier semaphores. Data moves between devices by JAX's collectives and lax.ppermute only.
A program may use at most 128 MiB of HBM per device.

v0:
```python
import functools
import math

import jax
import jax.numpy as jnp
from jax import lax
from jax.experimental import pallas as pl
from jax.experimental.pallas import tpu as pltpu
from jax.sharding import PartitionSpec as P


HEAD_DIM = 128
WINDOW = 2048
EPSILON = 1e-06
SELF_TILE = 256
VMEM_LIMIT = 24 * 2**20
CROSS_TILE = 256
LOG2E = 1.4426950408889634


def moved(block, axis, size, target):
    route = [(i, target(i)) for i in range(size)]
    route = [(i, j) for i, j in route if j is not None and 0 <= j < size]
    return lax.ppermute(block, axis, route)


def attend_kernel(
    place_ref, doc_ref, tail_ref, *refs, arrays, groups, sources, q_sources, tile, mode
):
    count = len(sources) * len(groups)
    q_refs, refs = refs[:arrays], refs[arrays:]
    kv_refs, refs = refs[:count], refs[count:]
    if mode == "finish":
        ml_in, acc_in, *old_refs = refs[: 2 + arrays]
        o_refs = refs[2 + arrays :]
    else:
        o_refs, states = refs[:arrays], refs[arrays:]
    rows = q_refs[0].shape[0]
    blocks = doc_ref.shape[0]
    factor = LOG2E / math.sqrt(HEAD_DIM)
    here = place_ref[0]
    parity = lax.rem(here, 2)

    def lanes(at):
        if isinstance(at, int):
            return slice(at * HEAD_DIM, (at + 1) * HEAD_DIM)
        return pl.ds(pl.multiple_of(at * HEAD_DIM, HEAD_DIM), HEAD_DIM)

    def block_of(source):
        if source[0] == "back":
            return here - source[1]
        if source[0] == "pair":
            return here + 1 - 2 * parity - source[1]
        return here - parity - 1 - source[1]

    def joined(key_block, query_block):
        safe = jnp.maximum(key_block, 0)
        wanted = jnp.logical_and(key_block >= 0, key_block < query_block)
        return jnp.logical_and(wanted, doc_ref[safe] == doc_ref[query_block])

    def live_rows(block):
        after = jnp.minimum(block + 1, blocks - 1)
        closing = jnp.logical_or(block == blocks - 1, doc_ref[after] != doc_ref[block])
        return jnp.where(closing, tail_ref[block], rows)

    def soften(q, spans, before):
        k = jnp.concatenate([k for k, _, _, _ in spans], axis=0)
        v = jnp.concatenate([v for _, v, _, _ in spans], axis=0)
        v = jnp.concatenate([v, jnp.ones(v.shape, v.dtype)], axis=1)
        s_all = lax.dot_general(q, k, (((1,), (1,)), ((), ())), preferred_element_type=jnp.float32)
        parts, at = [], 0
        m = None if before is None else before[0]
        for k, _, keep, open_span in spans:
            s = s_all[:, at : at + k.shape[0]]
            at += k.shape[0]
            if keep is not None:
                s = jnp.where(keep, s, -1e30)
            peak = jnp.max(s, axis=1, keepdims=True)
            if open_span is not None:
                peak = jnp.where(open_span, peak, -1e30)
            m = peak if m is None else jnp.maximum(m, peak)
            parts.append((s, open_span))
        weights = []
        for s, open_span in parts:
            top = m if open_span is None else jnp.where(open_span, m, 1e30)
            weights.append(jnp.exp2((s - top) * factor).astype(jnp.bfloat16))
        acc = jnp.dot(
            jnp.concatenate(weights, axis=1), v, preferred_element_type=jnp.float32
        )
        if before is not None:
            shrink = jnp.exp2((before[0] - m) * factor)
            return m, acc[:, HEAD_DIM:] + before[1] * shrink, acc[:, :HEAD_DIM] + before[2] * shrink
        return m, acc[:, HEAD_DIM:], acc[:, :HEAD_DIM]

    def state_lane(index):
        return lax.broadcasted_iota(jnp.int32, (tile, HEAD_DIM), 1) == index

    def over_heads(body):
        for g, (heads, shared) in enumerate(groups):
            slots = kv_refs[g * len(sources) : (g + 1) * len(sources)]
            kv_heads = slots[0].shape[1] // (2 * HEAD_DIM)

            def one(h, carry, g=g, heads=heads, shared=shared, slots=slots, kv_heads=kv_heads):
                at = 0 if shared else h

                def pick(slot, keys):
                    return slot[:keys, lanes(at)], slot[:keys, lanes(kv_heads + at)]

                body(slots, g * heads + h, pick)
                return carry

            lax.fori_loop(0, heads, one, 0)

    def begin(slots, head, pick):
        def visit(n, extra):
            query_block = block_of(q_sources[n])
            live = live_rows(query_block)
            for t in range(0, rows, tile):
                keys = t + tile
                row = t + lax.broadcasted_iota(jnp.int32, (tile, keys), 0)
                col = lax.broadcasted_iota(jnp.int32, (tile, keys), 1)
                keep = jnp.logical_and(col <= row, col < live)
                spans = [(*pick(slots[sources.index(q_sources[n])], keys), keep, None)]
                for slot, source in zip(slots, sources):
                    if source not in q_sources or source == extra:
                        spans.append((*pick(slot, rows), None, joined(block_of(source), query_block)))
                m, total, acc = soften(q_refs[n][t : t + tile, lanes(head)], spans, None)
                o_refs[n][t : t + tile, lanes(head)] = (acc / total).astype(jnp.bfloat16)
                if arrays == 1 or extra is None:
                    ml_out, acc_out = states
                    acc_out[t : t + tile, lanes(head)] = acc
                    kept = jnp.where(state_lane(2 * head), m, ml_out[t : t + tile, :])
                    ml_out[t : t + tile, :] = jnp.where(state_lane(2 * head + 1), total, kept)

        if arrays == 1:
            visit(0, None)
            return
        for first in (0, 1):

            @pl.when(parity == first)
            def _(first=first):
                visit(first, None)
                visit(1 - first, q_sources[first])

    def finish(slots, head, pick):
        for n, (q_ref, old_ref, o_ref) in enumerate(zip(q_refs, old_refs, o_refs)):

            def go(q_ref=q_ref, o_ref=o_ref, n=n):
                query_block = block_of(q_sources[n])
                for t in range(0, rows, tile):
                    ml = ml_in[t : t + tile, :]
                    before = [
                        jnp.sum(jnp.where(state_lane(2 * head + i), ml, 0.0), axis=1, keepdims=True)
                        for i in (0, 1)
                    ]
                    before.append(acc_in[t : t + tile, lanes(head)])
                    spans = [
                        (*pick(slot, rows), None, joined(block_of(source), query_block))
                        for slot, source in zip(slots, sources)
                    ]
                    _, total, acc = soften(q_ref[t : t + tile, lanes(head)], spans, before)
                    o_ref[t : t + tile, lanes(head)] = (acc / total).astype(jnp.bfloat16)

            if arrays == 1:
                go()
            else:
                pl.when(parity == n)(go)

                @pl.when(parity != n)
                def _(old_ref=old_ref, o_ref=o_ref):
                    o_ref[:, lanes(head)] = old_ref[:, lanes(head)]

    if mode == "begin":
        states[0][...] = jnp.zeros(states[0].shape, jnp.float32)
    over_heads(finish if mode == "finish" else begin)


def attend(scalars, q_list, kv_list, groups, sources, q_sources, tile, mode, state=()):
    rows, wide = q_list[0].shape
    arrays = len(q_list)
    smem = pl.BlockSpec(memory_space=pltpu.SMEM)
    vmem = pl.BlockSpec(memory_space=pltpu.VMEM)
    heads = sum(g[0] for g in groups)
    operands = [*q_list, *kv_list, *state]
    out_shape = [jax.ShapeDtypeStruct((rows, wide), jnp.bfloat16)] * arrays
    if mode == "begin":
        out_shape += [
            jax.ShapeDtypeStruct((rows, d * HEAD_DIM), jnp.float32) for d in (1, heads)
        ]
    return pl.pallas_call(
        functools.partial(
            attend_kernel,
            arrays=arrays,
            groups=tuple(groups),
            sources=tuple(sources),
            q_sources=tuple(q_sources),
            tile=min(tile, rows),
            mode=mode,
        ),
        out_shape=out_shape,
        in_specs=[smem] * len(scalars) + [vmem] * len(operands),
        out_specs=[vmem] * len(out_shape),
        compiler_params=pltpu.CompilerParams(vmem_limit_bytes=VMEM_LIMIT),
        name="attend",
    )(*scalars, *operands)


def project_call(places, base, pieces, w_blocks, first, out_type):
    rows, own = base.shape
    half = own // 2

    def kernel(places_ref, base_ref, *refs):
        near_refs, w_refs = refs[: len(pieces)], refs[len(pieces) : -2]
        o_ref, context_ref = refs[-2:]
        side = lax.rem(places_ref[0], 2)
        for step, ref in enumerate(near_refs):
            block, other = divmod(step, 2)
            at = block * own + (side if other == 0 else 1 - side) * half
            context_ref[:, pl.ds(pl.multiple_of(at, half), half)] = ref[...]
        total = base_ref[...].astype(jnp.float32)
        for block, w_ref in enumerate(w_refs):
            total += jnp.dot(
                context_ref[:, block * own : (block + 1) * own],
                w_ref[...],
                preferred_element_type=jnp.float32,
            )
        o_ref[...] = total.astype(o_ref.dtype)

    whole = lambda a: pl.BlockSpec(a.shape, lambda i, places_ref: (0, 0))
    corner = pl.BlockSpec((own, own), lambda i, places_ref: (0, places_ref[1] if first else 0))
    return pl.pallas_call(
        kernel,
        grid_spec=pltpu.PrefetchScalarGridSpec(
            num_scalar_prefetch=1,
            grid=(1,),
            in_specs=[whole(a) for a in (base, *pieces)]
            + [corner]
            + [whole(w) for w in w_blocks[1:]],
            out_specs=whole(base),
            scratch_shapes=[pltpu.VMEM((rows, own * len(w_blocks)), jnp.bfloat16)],
        ),
        out_shape=jax.ShapeDtypeStruct((rows, own), out_type),
        compiler_params=pltpu.CompilerParams(vmem_limit_bytes=VMEM_LIMIT),
        name="project",
    )(places, base, *pieces, *w_blocks)


def norm_into(lane, gain_ref, hidden_refs, normed_ref):
    wide = hidden_refs[0].shape[1]
    total = 0.0
    for ref in hidden_refs:
        x = ref[...].astype(jnp.float32)
        total += jnp.sum(x * x, axis=1, keepdims=True)
    scale = lax.rsqrt(total / (wide * len(hidden_refs)) + EPSILON)
    for step, ref in enumerate(hidden_refs):
        at = pl.multiple_of((lane ^ step) * wide, wide)
        x = ref[...].astype(jnp.float32)
        normed_ref[:, pl.ds(at, wide)] = (x * scale * gain_ref[:, pl.ds(at, wide)]).astype(
            jnp.bfloat16
        )


def fetch(place_ref, pieces, columns, buffer, sems, rings):
    z, y = place_ref[0] // 2, lax.rem(place_ref[0], 2)
    depth = buffer.shape[1] // 2
    order = []
    for k in range(rings):
        order.append(lax.rem(z - k + rings, rings))
        for t in (0, 1):
            rows = pl.ds(pl.multiple_of((y ^ t) * depth, depth), depth)

            def begin(name, slot=2 * k + t, k=k, rows=rows):
                ref, base = pieces[name]
                pltpu.make_async_copy(
                    ref.at[:, columns.start - base : columns.stop - base],
                    buffer.at[k, rows],
                    sems.at[slot],
                ).start()

            if k == 0:
                begin(("w", 0, t))
            else:

                @pl.when(z >= k)
                def _(k=k, t=t, begin=begin):
                    begin(("up", k, t))

                @pl.when(z < k)
                def _(k=k, t=t, begin=begin):
                    begin(("down", rings - k, t))

    return order


def gather_dot(normed_ref, order, pieces, columns, buffer, sems):
    total = 0.0
    first = pieces[("w", 0, 0)][0]
    depth = first.shape[0]
    for k, block in enumerate(order):
        for t in (0, 1):
            pltpu.make_async_copy(
                first.at[:, 0 : columns.stop - columns.start],
                buffer.at[k, pl.ds(t * depth, depth)],
                sems.at[2 * k + t],
            ).wait()
        at = pl.multiple_of(block * 2 * depth, 2 * depth)
        total += jnp.dot(
            normed_ref[:, pl.ds(at, 2 * depth)], buffer[k], preferred_element_type=jnp.float32
        )
    return total


def cache_call(place1, lane1, gain, hiddens, pieces, width, rings):
    names = list(pieces)
    rows, own = hiddens[0].shape
    depth = pieces[("w", 0, 0)][0].shape[0]
    groups = width // (2 * HEAD_DIM)
    columns = slice(0, width)

    def kernel(place_ref, lane_ref, gain_ref, *refs):
        hidden_refs = refs[: len(hiddens)]
        piece_refs = refs[len(hiddens) : len(hiddens) + len(names)]
        normed_ref, *cache_refs = refs[len(hiddens) + len(names) : -2]
        buffer, sems = refs[-2:]
        at = {n: (r, pieces[n][1]) for n, r in zip(names, piece_refs)}
        order = fetch(place_ref, at, columns, buffer, sems, rings)
        norm_into(lane_ref[0], gain_ref, hidden_refs, normed_ref)
        total = gather_dot(normed_ref, order, at, columns, buffer, sems)
        for g, ref in enumerate(cache_refs):
            for part in (0, 1):
                c = (part * groups + g) * HEAD_DIM
                ref[:, part * HEAD_DIM : (part + 1) * HEAD_DIM] = total[
                    :, c : c + HEAD_DIM
                ].astype(jnp.bfloat16)

    vmem = pl.BlockSpec(memory_space=pltpu.VMEM)
    smem = pl.BlockSpec(memory_space=pltpu.SMEM)
    return pl.pallas_call(
        kernel,
        out_shape=[jax.ShapeDtypeStruct((rows, own * len(hiddens)), jnp.bfloat16)]
        + [jax.ShapeDtypeStruct((rows, 2 * HEAD_DIM), jnp.bfloat16)] * groups,
        in_specs=[smem, smem, vmem]
        + [vmem] * len(hiddens)
        + [pl.BlockSpec(memory_space=pl.ANY)] * len(names),
        out_specs=[vmem] * (1 + groups),
        scratch_shapes=[
            pltpu.VMEM((rings, 2 * depth, width), jnp.bfloat16),
            pltpu.SemaphoreType.DMA((2 * rings,)),
        ],
        compiler_params=pltpu.CompilerParams(vmem_limit_bytes=VMEM_LIMIT),
        name="cache",
    )(place1, lane1, gain, *hiddens, *[pieces[n][0] for n in names])


def query_call(place1, normed, pieces, start, width, rings):
    names = list(pieces)
    rows = normed.shape[0]
    depth = pieces[("w", 0, 0)][0].shape[0]
    columns = slice(start, start + width)

    def kernel(place_ref, normed_ref, *refs):
        piece_refs = refs[: len(names)]
        o_ref, buffer, sems = refs[len(names) :]
        at = {n: (r, pieces[n][1]) for n, r in zip(names, piece_refs)}
        order = fetch(place_ref, at, columns, buffer, sems, rings)
        o_ref[...] = gather_dot(normed_ref, order, at, columns, buffer, sems).astype(jnp.bfloat16)

    vmem = pl.BlockSpec(memory_space=pltpu.VMEM)
    return pl.pallas_call(
        kernel,
        out_shape=jax.ShapeDtypeStruct((rows, width), jnp.bfloat16),
        in_specs=[pl.BlockSpec(memory_space=pltpu.SMEM), vmem]
        + [pl.BlockSpec(memory_space=pl.ANY)] * len(names),
        out_specs=vmem,
        scratch_shapes=[
            pltpu.VMEM((rings, 2 * depth, width), jnp.bfloat16),
            pltpu.SemaphoreType.DMA((2 * rings,)),
        ],
        compiler_params=pltpu.CompilerParams(vmem_limit_bytes=VMEM_LIMIT),
        name="queries",
    )(place1, normed, *[pieces[n][0] for n in names])


def paired_layer(
    residual,
    q_self,
    k_self,
    v_self,
    w_out,
    norm_gain,
    w_query,
    w_cache,
    block_doc,
    tail_len,
    *,
    seq,
    head,
):
    _, own = residual.shape
    half = own // 2
    parts = half // HEAD_DIM
    rings = seq // 2
    groups = w_cache.shape[1] // (2 * HEAD_DIM)
    place = lax.axis_index("seq").astype(jnp.int32)
    lane = lax.axis_index("head").astype(jnp.int32)
    side = lax.rem(place, 2)
    place1, lane1 = place[None], lane[None]

    def send(block, axis, target, source=None):
        size = seq if axis == "seq" else head
        return moved(
            block, axis, size, lambda i: target(i) if source is None or source(i) else None
        )

    up = lambda i: i + 2
    swap = lambda i: i ^ 1
    column = lambda a, at, size: lax.dynamic_slice_in_dim(a, at, size, 1)

    def kv_of(which):
        at = which * half
        return jnp.concatenate([column(k_self, at, half), column(v_self, at, half)], axis=1)

    mine, theirs = kv_of(side), kv_of(1 - side)
    q_mine = column(q_self, side * half, half)
    q_theirs = column(q_self, (1 - side) * half, half)
    above = send(mine, "seq", up)
    near = send(theirs, "seq", swap)
    across = send(near, "seq", up)
    odd = jnp.where(side == 1, above, across)
    far = send(odd, "seq", up, lambda i: i >= 2)
    q_near = send(q_theirs, "seq", swap)

    w_blocks = [w_out]
    late = lax.optimization_barrier(w_out)
    for step in (2, 1, 3):
        source = late if step == 1 else w_out
        piece = lax.dynamic_slice_in_dim(source, (lane ^ step) * own, own, 1)
        w_blocks.append(send(piece, "head", lambda i: i ^ step))

    wide = w_cache.shape[1]
    tables = []
    for name, w, base in (("c", w_cache, 0), ("q", w_query, wide)):
        table = {("w", 0, 0): (w, base)}
        table[("w", 0, 1)] = (send(w, "seq", swap), base)
        high = w
        for k in range(1, rings):
            if name == "q":
                high = send(high, "seq", up, lambda i: i // 2 >= k - 1)
            else:
                rises = lambda i: i // 2 + k < rings
                high = send(w, "seq", lambda i: i + 2 * k, rises)
            low = send(w, "seq", lambda i: i - 2 * k, lambda i: i // 2 >= k)
            table[("up", k, 0)] = (high, base)
            table[("down", k, 0)] = (low, base)
            risen = lambda i: i // 2 >= k
            fallen = lambda i: i // 2 < rings - k
            table[("up", k, 1)] = (send(high, "seq", swap, risen), base)
            table[("down", k, 1)] = (send(low, "seq", swap, fallen), base)
        tables.append(table)
    cache_pieces, query_pieces = tables

    scalars = (place1, block_doc, tail_len)
    pair = [("back", 0), ("pair", 0)]
    o_mine, o_theirs, *state = attend(
        scalars,
        [q_mine, q_near],
        [mine, near, above, across],
        [(parts, False)],
        pair + [("back", 2), ("pair", 2)],
        pair,
        SELF_TILE,
        "begin",
    )
    o_mine, o_theirs = attend(
        scalars,
        [q_mine, q_near],
        [far],
        [(parts, False)],
        [("odd", 2)],
        pair,
        SELF_TILE,
        "finish",
        [*state, o_mine, o_theirs],
    )
    both = lambda i: ((i // head) ^ 1) * head + ((i % head) ^ 2)
    route = [(i, both(i)) for i in range(seq * head)]
    corner = lax.ppermute(o_theirs, ("seq", "head"), route)
    flip = lambda i: i ^ 1
    places = jnp.stack([place, lane])
    contexts = [o_mine, send(o_theirs, "seq", swap), send(o_mine, "head", lambda i: i ^ 2), corner]
    others = [send(piece, "head", flip) for piece in contexts]
    partial = project_call(
        places,
        residual,
        contexts[:2] + others[:2],
        [w_blocks[0], w_blocks[2]],
        True,
        jnp.float32,
    )
    hidden = project_call(
        places,
        partial,
        contexts[2:] + others[2:],
        [w_blocks[1], w_blocks[3]],
        False,
        jnp.bfloat16,
    )
    hidden_x = send(hidden, "head", lambda i: i ^ 2)
    hidden_c = send(hidden, "head", lambda i: i ^ 1)
    hidden_xc = send(hidden_x, "head", lambda i: i ^ 1)
    normed, *caches = cache_call(
        place1,
        lane1,
        norm_gain[None, :],
        [hidden, hidden_c, hidden_x, hidden_xc],
        cache_pieces,
        wide,
        rings,
    )
    history = []
    for cache in caches:
        two = send(cache, "seq", up)
        chosen = jnp.where(side == 0, cache, two)
        one = send(chosen, "seq", swap)
        three = send(one, "seq", up)
        history.append([cache, two, one, three])
    cross_queries = query_call(place1, normed, query_pieces, wide, w_query.shape[1], rings)
    per = own // HEAD_DIM // groups
    shape = [(per, True)] * groups
    begun, *state = attend(
        scalars,
        [cross_queries],
        [slot for blocks in history for slot in blocks[:3]],
        shape,
        [("back", 0), ("back", 2), ("back", 1)],
        [("back", 0)],
        CROSS_TILE,
        "begin",
    )
    (cross_context,) = attend(
        scalars,
        [cross_queries],
        [blocks[3] for blocks in history],
        shape,
        [("back", 3)],
        [("back", 0)],
        CROSS_TILE,
        "finish",
        [*state, begun],
    )
    return (hidden, cross_context)


def direct_attend_kernel(
    place_ref, doc_ref, tail_ref, q_ref, *refs, slots, heads, group, q_tile, reach
):
    kv_refs = refs[: len(slots)]
    o_ref, m_ref, l_ref, acc_ref = refs[len(slots) :]
    rows = q_ref.shape[0]
    blocks = doc_ref.shape[0]
    kv_heads = heads // group
    factor = LOG2E / math.sqrt(HEAD_DIM)
    here = place_ref[0]
    own_doc = doc_ref[here]
    after = jnp.minimum(here + 1, blocks - 1)
    closing = jnp.logical_or(here == blocks - 1, doc_ref[after] != own_doc)
    live = jnp.where(closing, tail_ref[here], rows)

    def scores(kv_ref, t, h):
        q = q_ref[pl.ds(t, q_tile), h * HEAD_DIM : (h + 1) * HEAD_DIM]
        g = h // group
        k = kv_ref[:, g * HEAD_DIM : (g + 1) * HEAD_DIM]
        return lax.dot_general(q, k, (((1,), (1,)), ((), ())), preferred_element_type=jnp.float32)

    def values(kv_ref, h):
        g = kv_heads + h // group
        return kv_ref[:, g * HEAD_DIM : (g + 1) * HEAD_DIM]

    def tiles(step):
        def body(i, carry):
            step(pl.multiple_of(i * q_tile, q_tile))
            return carry

        lax.fori_loop(0, rows // q_tile, body, 0)

    def first(t):
        kv_ref = kv_refs[0]
        row = t + lax.broadcasted_iota(jnp.int32, (q_tile, rows), 0)
        col = lax.broadcasted_iota(jnp.int32, (q_tile, rows), 1)
        keep = jnp.logical_and(col <= row, col < live)
        for h in range(heads):
            s = jnp.where(keep, scores(kv_ref, t, h), -1e30)
            m = jnp.max(s, axis=1, keepdims=True)
            p = jnp.exp2((s - m) * factor)
            m_ref[h, pl.ds(t, q_tile), :] = jnp.broadcast_to(m, (q_tile, HEAD_DIM))
            l_ref[h, pl.ds(t, q_tile), :] = jnp.broadcast_to(
                jnp.sum(p, axis=1, keepdims=True), (q_tile, HEAD_DIM)
            )
            acc_ref[h, pl.ds(t, q_tile), :] = jnp.dot(
                p.astype(jnp.bfloat16), values(kv_ref, h), preferred_element_type=jnp.float32
            )

    def later(kv_ref, back):
        def step(t):
            if back * rows + rows - 1 >= reach:
                row = t + lax.broadcasted_iota(jnp.int32, (q_tile, rows), 0)
                col = lax.broadcasted_iota(jnp.int32, (q_tile, rows), 1)
                keep = back * rows + row - col < reach
            else:
                keep = None
            for h in range(heads):
                s = scores(kv_ref, t, h)
                if keep is not None:
                    s = jnp.where(keep, s, -1e30)
                m_old = m_ref[h, pl.ds(t, q_tile), :]
                m = jnp.maximum(m_old, jnp.max(s, axis=1, keepdims=True))
                shrink = jnp.exp2((m_old - m) * factor)
                p = jnp.exp2((s - m[:, :1]) * factor)
                m_ref[h, pl.ds(t, q_tile), :] = m
                l_ref[h, pl.ds(t, q_tile), :] = l_ref[h, pl.ds(t, q_tile), :] * shrink + jnp.sum(
                    p, axis=1, keepdims=True
                )
                acc_ref[h, pl.ds(t, q_tile), :] = acc_ref[
                    h, pl.ds(t, q_tile), :
                ] * shrink + jnp.dot(
                    p.astype(jnp.bfloat16), values(kv_ref, h), preferred_element_type=jnp.float32
                )

        return step

    tiles(first)
    for kv_ref, (even, odd) in zip(kv_refs[1:], slots[1:]):
        parity = lax.rem(here, 2)
        for back, only in ((even, 0), (odd, 1)):
            if back is None or (even == odd and only == 1):
                continue
            source = here - back
            wanted = jnp.logical_and(source >= 0, doc_ref[jnp.maximum(source, 0)] == own_doc)
            if even != odd:
                wanted = jnp.logical_and(wanted, parity == only)
            span = back

            @pl.when(wanted)
            def _(kv_ref=kv_ref, span=span):
                tiles(later(kv_ref, span))

    for h in range(heads):
        o_ref[:, h * HEAD_DIM : (h + 1) * HEAD_DIM] = (acc_ref[h] / l_ref[h]).astype(jnp.bfloat16)


def direct_attend(place, block_doc, tail_len, queries, column_block, heads, kv_list, slots, reach):
    rows, width = kv_list[0].shape
    kv_heads = width // (2 * HEAD_DIM)
    wide = heads * HEAD_DIM
    smem = pl.BlockSpec(memory_space=pltpu.SMEM)
    whole = pl.BlockSpec((rows, width), lambda i: (0, 0))
    return pl.pallas_call(
        functools.partial(
            direct_attend_kernel,
            slots=slots,
            heads=heads,
            group=heads // kv_heads,
            q_tile=min(256, rows),
            reach=reach,
        ),
        grid=(1,),
        out_shape=jax.ShapeDtypeStruct((rows, wide), jnp.bfloat16),
        in_specs=[smem, smem, smem, pl.BlockSpec((rows, wide), lambda i: (0, column_block))]
        + [whole] * len(kv_list),
        out_specs=pl.BlockSpec((rows, wide), lambda i: (0, 0)),
        scratch_shapes=[pltpu.VMEM((heads, rows, HEAD_DIM), jnp.float32)] * 3,
        compiler_params=pltpu.CompilerParams(vmem_limit_bytes=VMEM_LIMIT),
        name="attend",
    )(place, block_doc, tail_len, queries, *kv_list)


def direct_project_kernel(*refs, parts, blocks):
    residual_ref = refs[0]
    context_refs = refs[1 : 1 + parts * blocks]
    w_refs = refs[1 + parts * blocks : 1 + parts * blocks + blocks]
    o_ref = refs[-1]
    total = residual_ref[...].astype(jnp.float32)
    depth = context_refs[0].shape[1]
    for part in range(parts):
        for block in range(blocks):
            total += jnp.dot(
                context_refs[part * blocks + block][...],
                w_refs[block][part * depth : (part + 1) * depth, :],
                preferred_element_type=jnp.float32,
            )
    o_ref[...] = total.astype(jnp.bfloat16)


def norm_kernel(place_ref, gain_ref, *refs, near):
    hidden_refs, o_ref = refs[:-1], refs[-1]
    wide = hidden_refs[0].shape[1]
    total = 0.0
    for ref in hidden_refs:
        x = ref[...].astype(jnp.float32)
        total += jnp.sum(x * x, axis=1, keepdims=True)
    scale = lax.rsqrt(total / (wide * len(hidden_refs)) + EPSILON)
    for step, ref in enumerate(hidden_refs):
        at = pl.multiple_of(near(place_ref[0], step) * wide, wide)
        x = ref[...].astype(jnp.float32)
        o_ref[:, pl.ds(at, wide)] = (x * scale * gain_ref[:, pl.ds(at, wide)]).astype(jnp.bfloat16)


def columns_kernel(order_ref, normed_ref, *refs):
    w_refs, o_ref = refs[:-1], refs[-1]
    depth = w_refs[0].shape[0]
    total = 0.0
    for step, ref in enumerate(w_refs):
        at = pl.multiple_of(order_ref[step] * depth, depth)
        total += jnp.dot(
            normed_ref[:, pl.ds(at, depth)], ref[...], preferred_element_type=jnp.float32
        )
    o_ref[...] = total.astype(jnp.bfloat16)


def simple_call(kernel, out_shape, scalars, arrays):
    return pl.pallas_call(
        kernel,
        out_shape=out_shape,
        in_specs=[pl.BlockSpec(memory_space=pltpu.SMEM)] * len(scalars)
        + [pl.BlockSpec(memory_space=pltpu.VMEM)] * len(arrays),
        out_specs=pl.BlockSpec(memory_space=pltpu.VMEM),
        compiler_params=pltpu.CompilerParams(vmem_limit_bytes=VMEM_LIMIT),
    )(*scalars, *arrays)


def direct_layer(
    residual,
    q_self,
    k_self,
    v_self,
    w_out,
    norm_gain,
    w_query,
    w_cache,
    block_doc,
    tail_len,
    *,
    seq,
    head,
    span,
    paired,
):
    rows, own = residual.shape
    local_heads = q_self.shape[1] // HEAD_DIM
    place = lax.axis_index("seq").astype(jnp.int32)
    lane = lax.axis_index("head").astype(jnp.int32)
    place1, lane1 = place[None], lane[None]

    def along(block, target):
        return moved(block, "seq", seq, target)

    def across(block, step):
        return moved(block, "head", head, lambda i: i ^ step)

    even = lambda i: i % 2 == 0

    def spread(block):
        if not paired:
            return [along(block, lambda i, d=d: i + d) for d in range(1, span)]
        far = along(block, lambda i: i + 2)
        near = along(block, lambda i: i + 1 if even(i) else None)
        swap = along(far, lambda i: i ^ 1)
        last = along(swap, lambda i: i + 2 if even(i) else None)
        return [far, near, swap, last]

    if paired:
        slots = ((0, 0), (2, 2), (None, 1), (1, 3), (3, None))
    else:
        slots = tuple((d, d) for d in range(span))

    parts = local_heads // 2
    per = local_heads // parts
    width = per * HEAD_DIM
    kv_parts = []
    for c in range(parts):
        cols = slice(c * width, (c + 1) * width)
        own_kv = jnp.concatenate([k_self[:, cols], v_self[:, cols]], axis=1)
        kv_parts.append([own_kv] + spread(own_kv))

    w_blocks = []
    for step in range(head):
        piece = lax.dynamic_slice_in_dim(w_out, (lane ^ step) * own, own, 1)
        w_blocks.append(piece if step == 0 else across(piece, step))

    def gathered(w):
        if not paired:
            whole = lax.all_gather(w, "seq", axis=0, tiled=True)
            return [whole]
        pieces = [w, along(w, lambda i: i ^ 1)]
        ring = list(pieces)
        for distance in range(1, seq // 2):
            if distance <= seq // 4:
                ring = [along(p, lambda i: (i - 2) % seq) for p in ring]
                pieces += ring
            else:
                pieces += [
                    along(p, lambda i: (i + 2 * (seq // 2 - distance)) % seq) for p in pieces[:2]
                ]
        return pieces

    if paired:
        order = [(place ^ y) + 2 * distance for distance in range(seq // 2) for y in (0, 1)]
        order = jnp.stack([lax.rem(o, seq) for o in order])
    else:
        order = jnp.zeros((1,), jnp.int32)
    cache_w = gathered(w_cache)
    query_w = gathered(w_query)

    contexts = []
    for c in range(parts):
        mine = direct_attend(
            place1, block_doc, tail_len, q_self, c, per, kv_parts[c], slots, WINDOW
        )
        pair = [mine, across(mine, 2)]
        other = [across(p, 1) for p in pair]
        contexts += [pair[0], other[0], pair[1], other[1]]
    hidden = simple_call(
        functools.partial(direct_project_kernel, parts=parts, blocks=head),
        jax.ShapeDtypeStruct((rows, own), jnp.bfloat16),
        [],
        [residual, *contexts, *w_blocks],
    )
    pair = [hidden, across(hidden, 2)]
    other = [across(p, 1) for p in pair]
    normed = simple_call(
        functools.partial(norm_kernel, near=lambda at, step: at ^ step),
        jax.ShapeDtypeStruct((rows, own * head), jnp.bfloat16),
        [lane1],
        [norm_gain[None, :], pair[0], other[0], pair[1], other[1]],
    )
    cache = simple_call(
        columns_kernel,
        jax.ShapeDtypeStruct((rows, w_cache.shape[1]), jnp.bfloat16),
        [order],
        [normed, *cache_w],
    )
    history = [cache] + spread(cache)
    cross_queries = simple_call(
        columns_kernel,
        jax.ShapeDtypeStruct((rows, w_query.shape[1]), jnp.bfloat16),
        [order],
        [normed, *query_w],
    )
    cross_context = direct_attend(
        place1,
        block_doc,
        tail_len,
        cross_queries,
        0,
        local_heads,
        history,
        slots,
        rows * span,
    )
    return (hidden, cross_context)


def solution(mesh):
    seq, head = mesh.shape["seq"], mesh.shape["head"]
    span = min(5, seq // 2)
    in_specs = (
        P("seq", "head"),
        P("seq", "head"),
        P("seq", "head"),
        P("seq", "head"),
        P("head", None),
        P(),
        P("seq", "head"),
        P("seq", "head"),
        P(),
        P(),
    )
    out_specs = (P("seq", "head"), P("seq", "head"))
    if seq == 2 * span and head == 4:
        layer = functools.partial(paired_layer, seq=seq, head=head)
    else:
        layer = functools.partial(direct_layer, seq=seq, head=head, span=span, paired=False)

    def body(*args):
        return layer(*args)

    return jax.shard_map(body, mesh=mesh, in_specs=in_specs, out_specs=out_specs, check_vma=False)
```

profile of v0, /device:TPU:0, one launch (start us, length us, event | category | flops | bytes accessed | tf_op | source)
XLA Modules:
  0.0 317.3 jit_solution(2819906303181098150)
XLA Ops:
  8.9 14.0 %collective-permute-done.2.refs_3_ = bf16[512,768]{1,0:T(8,128)(2,1)} collective-permute-done((bf16[512,768]{1,0:T(8,128)(2,1)S(1)}, bf16[512,768]{1,0:T(8,128)(2,1)}, u32[]{:S(2)}, u32[]{:S(2)}) %collective-permute-start.2) | collective-permute-done | bytes 786464 | tf_op jit(solution)/shard_map/ppermute | solution.py:24
  23.0 3.7 %collective-permute-start.3 = (bf16[512,768]{1,0:T(8,128)(2,1)}, bf16[512,768]{1,0:T(8,128)(2,1)S(1)}, u32[]{:S(2)}, u32[]{:S(2)}) collective-permute-start(bf16[512,768]{1,0:T(8,128)(2,1)} %collective-permute-done.2.refs_3_), channel_id=1, source_target_pairs={{0,8},{4,12},{8,16},{12,20},{16,24},{20,28},{1,9},{5,13},{9,17},{1... | collective-permute-start | bytes 2359304 | tf_op jit(solution)/shard_map/ppermute | solution.py:24
  29.1 13.8 %collective-permute-done.3.refs_5_ = bf16[512,768]{1,0:T(8,128)(2,1)S(1)} collective-permute-done((bf16[512,768]{1,0:T(8,128)(2,1)}, bf16[512,768]{1,0:T(8,128)(2,1)S(1)}, u32[]{:S(2)}, u32[]{:S(2)}) %collective-permute-start.3) | collective-permute-done | bytes 786464 | tf_op jit(solution)/shard_map/ppermute | solution.py:24
  52.8 7.1 %collective-permute-start.19 = (bf16[384,512]{1,0:T(8,128)(2,1)}, bf16[384,512]{1,0:T(8,128)(2,1)S(1)}, u32[]{:S(2)}, u32[]{:S(2)}) collective-permute-start(bf16[384,512]{1,0:T(8,128)(2,1)} %refs_4_.3), channel_id=1, source_target_pairs={{0,8},{4,12},{8,16},{12,20},{16,24},{20,28},{1,9},{5,13},{9,17},{1... | collective-permute-start | bytes 1179656 | tf_op jit(solution)/shard_map/ppermute | solution.py:24
  60.4 8.3 %collective-permute-done.19.refs_6_ = bf16[384,512]{1,0:T(8,128)(2,1)S(1)} collective-permute-done((bf16[384,512]{1,0:T(8,128)(2,1)}, bf16[384,512]{1,0:T(8,128)(2,1)S(1)}, u32[]{:S(2)}, u32[]{:S(2)}) %collective-permute-start.19) | collective-permute-done | bytes 393248 | tf_op jit(solution)/shard_map/ppermute | solution.py:24
  70.0 9.2 %collective-permute-start.23 = (bf16[384,512]{1,0:T(8,128)(2,1)}, bf16[384,512]{1,0:T(8,128)(2,1)S(1)}, u32[]{:S(2)}, u32[]{:S(2)}) collective-permute-start(bf16[384,512]{1,0:T(8,128)(2,1)} %refs_4_.3), channel_id=1, source_target_pairs={{0,16},{4,20},{8,24},{12,28},{1,17},{5,21},{9,25},{13,29},{2,18},{... | collective-permute-start | bytes 1179656 | tf_op jit(solution)/shard_map/ppermute | solution.py:24
  79.2 11.7 %attend.4 = (bf16[512,384]{1,0:T(8,128)(2,1)S(1)}, bf16[512,384]{1,0:T(8,128)(2,1)S(1)}, f32[512,128]{1,0:T(8,128)S(1)}, f32[512,384]{1,0:T(8,128)S(1)}) custom-call(s32[1]{0:T(128)} %bitcast.place_ref, s32[8]{0:T(128)S(1)} %copy-done.11, s32[8]{0:T(128)S(1)} %copy-done.12, bf16[512,384]{1,0:T(8,128)(2,1)S(1)} %get-tuple-element.33.refs_0_, ...), custom_call_target="tpu_custom_call" | custom-call | tf_op jit(solution)/shard_map/attend/pallas_call | solution.py:190
  90.9 3.7 %attend.5 = (bf16[512,384]{1,0:T(8,128)(2,1)S(1)}, bf16[512,384]{1,0:T(8,128)(2,1)S(1)}) custom-call(s32[1]{0:T(128)} %bitcast.place_ref, s32[8]{0:T(128)S(1)} %copy-done.11, s32[8]{0:T(128)S(1)} %copy-done.12, bf16[512,384]{1,0:T(8,128)(2,1)S(1)} %get-tuple-element.33.refs_0_, bf16[512,384]{1,0:T(8,128)(2,1)} %collective-permute-done.refs_1_, ...), custom_call_target="tpu_custom_call" | custom-call | tf_op jit(solution)/shard_map/attend/pallas_call | solution.py:190
  98.2 4.5 %collective-permute-done.5.refs_1_ = bf16[512,384]{1,0:T(8,128)(2,1)S(1)} collective-permute-done((bf16[512,384]{1,0:T(8,128)(2,1)S(1)}, bf16[512,384]{1,0:T(8,128)(2,1)S(1)}, u32[]{:S(2)}, u32[]{:S(2)}) %collective-permute-start.5) | collective-permute-done | bytes 393248 | tf_op jit(solution)/shard_map/ppermute | solution.py:24
  102.7 11.1 %collective-permute-done.9.refs_0_ = bf16[512,384]{1,0:T(8,128)(2,1)S(1)} collective-permute-done((bf16[512,384]{1,0:T(8,128)(2,1)S(1)}, bf16[512,384]{1,0:T(8,128)(2,1)S(1)}, u32[]{:S(2)}, u32[]{:S(2)}) %collective-permute-start.9) | collective-permute-done | bytes 393248 | tf_op jit(solution)/shard_map/ppermute | solution.py:24
  113.9 7.6 %collective-permute-done.10.refs_1_ = bf16[512,384]{1,0:T(8,128)(2,1)S(1)} collective-permute-done((bf16[512,384]{1,0:T(8,128)(2,1)S(1)}, bf16[512,384]{1,0:T(8,128)(2,1)S(1)}, u32[]{:S(2)}, u32[]{:S(2)}) %collective-permute-start.10) | collective-permute-done | bytes 393248 | tf_op jit(solution)/shard_map/ppermute | solution.py:487
  124.4 7.9 %collective-permute-start.32 = (bf16[384,768]{1,0:T(8,128)(2,1)S(1)}, bf16[384,768]{1,0:T(8,128)(2,1)}, u32[]{:S(2)}, u32[]{:S(2)}) collective-permute-start(bf16[384,768]{1,0:T(8,128)(2,1)S(1)} %copy-done.4), channel_id=1, source_target_pairs={{0,8},{4,12},{8,16},{12,20},{16,24},{20,28},{1,9},{5,13},{9,17},{1... | collective-permute-start | bytes 1769480 | tf_op jit(solution)/shard_map/ppermute | solution.py:24
  143.6 11.4 %collective-permute-done.24.refs_11_ = bf16[384,512]{1,0:T(8,128)(2,1)S(1)} collective-permute-done((bf16[384,512]{1,0:T(8,128)(2,1)}, bf16[384,512]{1,0:T(8,128)(2,1)S(1)}, u32[]{:S(2)}, u32[]{:S(2)}) %collective-permute-start.24) | collective-permute-done | bytes 393248 | tf_op jit(solution)/shard_map/ppermute | solution.py:24
  166.0 5.0 %collective-permute-done.22.refs_9_ = bf16[384,512]{1,0:T(8,128)(2,1)S(1)} collective-permute-done((bf16[384,512]{1,0:T(8,128)(2,1)S(1)}, bf16[384,512]{1,0:T(8,128)(2,1)S(1)}, u32[]{:S(2)}, u32[]{:S(2)}) %collective-permute-start.22) | collective-permute-done | bytes 393248 | tf_op jit(solution)/shard_map/ppermute | solution.py:24
  182.9 7.0 %collective-permute-done.30.refs_17_ = bf16[384,512]{1,0:T(8,128)(2,1)S(1)} collective-permute-done((bf16[384,512]{1,0:T(8,128)(2,1)S(1)}, bf16[384,512]{1,0:T(8,128)(2,1)S(1)}, u32[]{:S(2)}, u32[]{:S(2)}) %collective-permute-start.30) | collective-permute-done | bytes 393248 | tf_op jit(solution)/shard_map/ppermute | solution.py:24
  196.5 5.6 %cache.1 = (bf16[512,3072]{1,0:T(8,128)(2,1)S(1)}, bf16[512,256]{1,0:T(8,128)(2,1)S(1)}, bf16[512,256]{1,0:T(8,128)(2,1)}) custom-call(s32[1]{0:T(128)} %bitcast.place_ref, s32[1]{0:T(128)} %bitcast.1.lane_ref, f32[1,3072]{1,0:T(1,128)S(1)} %bitcast.5, bf16[512,768]{1,0:T(8,128)(2,1)S(1)} %copy-done, bf16[512,768]{1,0:T(8,128)(2,1)S(1)} %collective-permute-done.15.refs_1_, ...), custom_call_target="tpu_custom_call" | custom-call | tf_op jit(solution)/shard_map/cache/pallas_call | solution.py:338
  202.1 3.7 %collective-permute-start.44 = (bf16[512,256]{1,0:T(8,128)(2,1)S(1)}, bf16[512,256]{1,0:T(8,128)(2,1)S(1)}, u32[]{:S(2)}, u32[]{:S(2)}) collective-permute-start(bf16[512,256]{1,0:T(8,128)(2,1)S(1)} %get-tuple-element.21.refs_1_), channel_id=1, source_target_pairs={{0,8},{4,12},{8,16},{12,20},{16,24},{20,28},{1,9},{5,13},{9,17},{1... | collective-permute-start | bytes 786440 | tf_op jit(solution)/shard_map/ppermute | solution.py:24
  205.8 34.3 %collective-permute-done.37.refs_7_ = bf16[384,768]{1,0:T(8,128)(2,1)} collective-permute-done((bf16[384,768]{1,0:T(8,128)(2,1)S(1)}, bf16[384,768]{1,0:T(8,128)(2,1)}, u32[]{:S(2)}, u32[]{:S(2)}) %collective-permute-start.37) | collective-permute-done | bytes 589856 | tf_op jit(solution)/shard_map/ppermute | solution.py:24
  248.8 4.5 %collective-permute-start.43 = (bf16[384,768]{1,0:T(8,128)(2,1)}, bf16[384,768]{1,0:T(8,128)(2,1)S(1)}, u32[]{:S(2)}, u32[]{:S(2)}) collective-permute-start(bf16[384,768]{1,0:T(8,128)(2,1)} %copy-done.8), channel_id=1, source_target_pairs={{0,4},{4,0},{1,5},{5,1},{2,6},{6,2},{3,7},{7,3}} | collective-permute-start | bytes 1769480 | tf_op jit(solution)/shard_map/ppermute | solution.py:24
  260.1 11.1 %collective-permute-done.39.refs_9_ = bf16[384,768]{1,0:T(8,128)(2,1)} collective-permute-done((bf16[384,768]{1,0:T(8,128)(2,1)}, bf16[384,768]{1,0:T(8,128)(2,1)}, u32[]{:S(2)}, u32[]{:S(2)}) %collective-permute-start.39) | collective-permute-done | bytes 589856 | tf_op jit(solution)/shard_map/ppermute | solution.py:24
  272.7 16.6 %collective-permute-done.45.refs_3_ = bf16[512,256]{1,0:T(8,128)(2,1)S(1)} collective-permute-done((bf16[512,256]{1,0:T(8,128)(2,1)S(1)}, bf16[512,256]{1,0:T(8,128)(2,1)S(1)}, u32[]{:S(2)}, u32[]{:S(2)}) %collective-permute-start.45) | collective-permute-done | bytes 262176 | tf_op jit(solution)/shard_map/ppermute | solution.py:24
  295.8 4.4 %queries.1.refs_0_ = bf16[512,768]{1,0:T(8,128)(2,1)S(1)} custom-call(s32[1]{0:T(128)} %bitcast.place_ref, bf16[512,3072]{1,0:T(8,128)(2,1)S(1)} %get-tuple-element.20.normed_ref, bf16[384,768]{1,0:T(8,128)(2,1)S(1)} %copy-done.5, bf16[384,768]{1,0:T(8,128)(2,1)S(1)} %copy-done.7, bf16[384,768]{1,0:T(8,128)(2,1)} %collective-permute-done.32.refs_2_, ...), custom_call_target="tpu_custom_call" | custom-call | tf_op jit(solution)/shard_map/queries/pallas_call | solution.py:369
  300.3 11.2 %attend.6 = (bf16[512,768]{1,0:T(8,128)(2,1)S(1)}, f32[512,128]{1,0:T(8,128)S(1)}, f32[512,768]{1,0:T(8,128)S(1)}) custom-call(s32[1]{0:T(128)} %bitcast.place_ref, s32[8]{0:T(128)S(1)} %copy-done.11, s32[8]{0:T(128)S(1)} %copy-done.12, bf16[512,768]{1,0:T(8,128)(2,1)S(1)} %queries.1.refs_0_, bf16[512,256]{1,0:T(8,128)(2,1)S(1)} %get-tuple-element.21.refs_1_, ...), custom_call_target="tpu_custom_call" | custom-call | tf_op jit(solution)/shard_map/attend/pallas_call | solution.py:190
  311.5 5.9 %attend.7 = bf16[512,768]{1,0:T(8,128)(2,1)} custom-call(s32[1]{0:T(128)} %bitcast.place_ref, s32[8]{0:T(128)S(1)} %copy-done.11, s32[8]{0:T(128)S(1)} %copy-done.12, bf16[512,768]{1,0:T(8,128)(2,1)S(1)} %queries.1.refs_0_, bf16[512,256]{1,0:T(8,128)(2,1)S(1)} %collective-permute-done.46.refs_1_, bf16[512,256]{1,0:T(8,128)(2,1)S(1)} %collective-permute-done.49.refs_2_, ...), custom_call_target="tpu_custom_call" | custom-call | tf_op jit(solution)/shard_map/attend/pallas_call | solution.py:190
  (127 shorter events, 92.7 us)
Async XLA Ops:
  27.6 25.2 %collective-permute-start = (bf16[512,384]{1,0:T(8,128)(2,1)}, bf16[512,384]{1,0:T(8,128)(2,1)}, u32[]{:S(2)}, u32[]{:S(2)}) collective-permute-start(bf16[512,384]{1,0:T(8,128)(2,1)} %get-tuple-element.32), channel_id=1, source_target_pairs={{0,4},{4,0},{8,12},{12,8},{16,20},{20,16},{24,28},{28,24},{1,5},{5... | collective-permute-start | bytes 1179656 | tf_op jit(solution)/shard_map/ppermute | solution.py:24
  43.9 26.1 %collective-permute-start.4 = (bf16[512,768]{1,0:T(8,128)(2,1)}, bf16[512,768]{1,0:T(8,128)(2,1)}, u32[]{:S(2)}, u32[]{:S(2)}) collective-permute-start(bf16[512,768]{1,0:T(8,128)(2,1)} %broadcast_select_fusion), channel_id=1, source_target_pairs={{8,16},{12,20},{16,24},{20,28},{9,17},{13,21},{17,25},{21,29},{10,... | collective-permute-start | bytes 2359304 | tf_op jit(solution)/shard_map/ppermute | solution.py:24
  47.8 50.0 %collective-permute-start.8 = (bf16[768,768]{1,0:T(8,128)(2,1)}, bf16[768,768]{1,0:T(8,128)(2,1)}, u32[]{:S(2)}, u32[]{:S(2)}) collective-permute-start(bf16[768,768]{1,0:T(8,128)(2,1)} %constant_dynamic-slice_fusion.2), channel_id=1, source_target_pairs={{0,1},{1,0},{2,3},{3,2},{4,5},{5,4},{6,7},{7,6},{8,9},{9,8},{10,11... | collective-permute-start | bytes 3538952 | tf_op jit(solution)/shard_map/ppermute | solution.py:24
  51.2 47.0 %collective-permute-start.13 = (bf16[768,768]{1,0:T(8,128)(2,1)S(1)}, bf16[768,768]{1,0:T(8,128)(2,1)S(1)}, u32[]{:S(2)}, u32[]{:S(2)}) collective-permute-start(bf16[768,768]{1,0:T(8,128)(2,1)S(1)} %get-tuple-element.27), channel_id=1, source_target_pairs={{0,2},{1,3},{2,0},{3,1},{4,6},{5,7},{6,4},{7,5},{8,10},{9,11},{10,... | collective-permute-start | bytes 3538952 | tf_op jit(solution)/shard_map/ppermute | solution.py:24
  59.9 61.6 %collective-permute-start.14 = (bf16[768,768]{1,0:T(8,128)(2,1)S(1)}, bf16[768,768]{1,0:T(8,128)(2,1)S(1)}, u32[]{:S(2)}, u32[]{:S(2)}) collective-permute-start(bf16[768,768]{1,0:T(8,128)(2,1)S(1)} %get-tuple-element.26), channel_id=1, source_target_pairs={{0,3},{1,2},{2,1},{3,0},{4,7},{5,6},{6,5},{7,4},{8,11},{9,10},{10,... | collective-permute-start | bytes 3538952 | tf_op jit(solution)/shard_map/ppermute | solution.py:24
  68.7 26.0 %collective-permute-start.20 = (bf16[384,512]{1,0:T(8,128)(2,1)}, bf16[384,512]{1,0:T(8,128)(2,1)S(1)}, u32[]{:S(2)}, u32[]{:S(2)}) collective-permute-start(bf16[384,512]{1,0:T(8,128)(2,1)} %refs_4_.3), channel_id=1, source_target_pairs={{8,0},{12,4},{16,8},{20,12},{24,16},{28,20},{9,1},{13,5},{17,9},{2... | collective-permute-start | bytes 1179656 | tf_op jit(solution)/shard_map/ppermute | solution.py:24
  70.0 26.3 %collective-permute-start.23 = (bf16[384,512]{1,0:T(8,128)(2,1)}, bf16[384,512]{1,0:T(8,128)(2,1)S(1)}, u32[]{:S(2)}, u32[]{:S(2)}) collective-permute-start(bf16[384,512]{1,0:T(8,128)(2,1)} %refs_4_.3), channel_id=1, source_target_pairs={{0,16},{4,20},{8,24},{12,28},{1,17},{5,21},{9,25},{13,29},{2,18},{... | collective-permute-start | bytes 1179656 | tf_op jit(solution)/shard_map/ppermute | solution.py:24
  97.7 23.7 %collective-permute-start.10 = (bf16[512,384]{1,0:T(8,128)(2,1)S(1)}, bf16[512,384]{1,0:T(8,128)(2,1)S(1)}, u32[]{:S(2)}, u32[]{:S(2)}) collective-permute-start(bf16[512,384]{1,0:T(8,128)(2,1)S(1)} %get-tuple-element.19), channel_id=1, source_target_pairs={{0,6},{1,7},{2,4},{3,5},{4,2},{5,3},{6,0},{7,1},{8,14},{9,15},{10,... | collective-permute-start | bytes 1179656 | tf_op jit(solution)/shard_map/ppermute | solution.py:487
  98.2 24.5 %collective-permute-start.6 = (bf16[512,384]{1,0:T(8,128)(2,1)S(1)}, bf16[512,384]{1,0:T(8,128)(2,1)S(1)}, u32[]{:S(2)}, u32[]{:S(2)}) collective-permute-start(bf16[512,384]{1,0:T(8,128)(2,1)S(1)} %get-tuple-element.18.refs_0_), channel_id=1, source_target_pairs={{0,1},{1,0},{2,3},{3,2},{4,5},{5,4},{6,7},{7,6},{8,9},{9,8},{10,11... | collective-permute-start | bytes 1179656 | tf_op jit(solution)/shard_map/ppermute | solution.py:24
  121.5 33.5 %collective-permute-start.24 = (bf16[384,512]{1,0:T(8,128)(2,1)}, bf16[384,512]{1,0:T(8,128)(2,1)S(1)}, u32[]{:S(2)}, u32[]{:S(2)}) collective-permute-start(bf16[384,512]{1,0:T(8,128)(2,1)} %refs_4_.3), channel_id=1, source_target_pairs={{16,0},{20,4},{24,8},{28,12},{17,1},{21,5},{25,9},{29,13},{18,2},{... | collective-permute-start | bytes 1179656 | tf_op jit(solution)/shard_map/ppermute | solution.py:24
  122.8 37.8 %collective-permute-start.31 = (bf16[384,768]{1,0:T(8,128)(2,1)S(1)}, bf16[384,768]{1,0:T(8,128)(2,1)S(1)}, u32[]{:S(2)}, u32[]{:S(2)}) collective-permute-start(bf16[384,768]{1,0:T(8,128)(2,1)S(1)} %copy-done.4), channel_id=1, source_target_pairs={{0,4},{4,0},{8,12},{12,8},{16,20},{20,16},{24,28},{28,24},{1,5},{5... | collective-permute-start | bytes 1769480 | tf_op jit(solution)/shard_map/ppermute | solution.py:24
  124.4 37.7 %collective-permute-start.32 = (bf16[384,768]{1,0:T(8,128)(2,1)S(1)}, bf16[384,768]{1,0:T(8,128)(2,1)}, u32[]{:S(2)}, u32[]{:S(2)}) collective-permute-start(bf16[384,768]{1,0:T(8,128)(2,1)S(1)} %copy-done.4), channel_id=1, source_target_pairs={{0,8},{4,12},{8,16},{12,20},{16,24},{20,28},{1,9},{5,13},{9,17},{1... | collective-permute-start | bytes 1769480 | tf_op jit(solution)/shard_map/ppermute | solution.py:24
  132.3 24.1 %collective-permute-start.27 = (bf16[384,512]{1,0:T(8,128)(2,1)}, bf16[384,512]{1,0:T(8,128)(2,1)S(1)}, u32[]{:S(2)}, u32[]{:S(2)}) collective-permute-start(bf16[384,512]{1,0:T(8,128)(2,1)} %refs_4_.3), channel_id=1, source_target_pairs={{0,24},{4,28},{1,25},{5,29},{2,26},{6,30},{3,27},{7,31}} | collective-permute-start | bytes 1179656 | tf_op jit(solution)/shard_map/ppermute | solution.py:24
  164.5 26.6 %collective-permute-start.36 = (bf16[384,768]{1,0:T(8,128)(2,1)}, bf16[384,768]{1,0:T(8,128)(2,1)}, u32[]{:S(2)}, u32[]{:S(2)}) collective-permute-start(bf16[384,768]{1,0:T(8,128)(2,1)} %collective-permute-done.32.refs_2_), channel_id=1, source_target_pairs={{8,16},{12,20},{16,24},{20,28},{9,17},{13,21},{17,25},{21,29},{10,... | collective-permute-start | bytes 1769480 | tf_op jit(solution)/shard_map/ppermute | solution.py:24
  189.8 50.3 %collective-permute-start.37 = (bf16[384,768]{1,0:T(8,128)(2,1)S(1)}, bf16[384,768]{1,0:T(8,128)(2,1)}, u32[]{:S(2)}, u32[]{:S(2)}) collective-permute-start(bf16[384,768]{1,0:T(8,128)(2,1)S(1)} %copy-done.4), channel_id=1, source_target_pairs={{16,0},{20,4},{24,8},{28,12},{17,1},{21,5},{25,9},{29,13},{18,2},{... | collective-permute-start | bytes 1769480 | tf_op jit(solution)/shard_map/ppermute | solution.py:24
  191.1 52.5 %collective-permute-start.41 = (bf16[384,768]{1,0:T(8,128)(2,1)S(1)}, bf16[384,768]{1,0:T(8,128)(2,1)S(1)}, u32[]{:S(2)}, u32[]{:S(2)}) collective-permute-start(bf16[384,768]{1,0:T(8,128)(2,1)S(1)} %copy-done.4), channel_id=1, source_target_pairs={{24,0},{28,4},{25,1},{29,5},{26,2},{30,6},{27,3},{31,7}} | collective-permute-start | bytes 1769480 | tf_op jit(solution)/shard_map/ppermute | solution.py:24
  192.4 56.4 %collective-permute-start.34 = (bf16[384,768]{1,0:T(8,128)(2,1)}, bf16[384,768]{1,0:T(8,128)(2,1)}, u32[]{:S(2)}, u32[]{:S(2)}) collective-permute-start(bf16[384,768]{1,0:T(8,128)(2,1)} %collective-permute-done.32.refs_2_), channel_id=1, source_target_pairs={{8,12},{12,8},{16,20},{20,16},{24,28},{28,24},{9,13},{13,9},{17,21... | collective-permute-start | bytes 1769480 | tf_op jit(solution)/shard_map/ppermute | solution.py:24
  193.9 59.3 %collective-permute-start.40 = (bf16[384,768]{1,0:T(8,128)(2,1)}, bf16[384,768]{1,0:T(8,128)(2,1)}, u32[]{:S(2)}, u32[]{:S(2)}) collective-permute-start(bf16[384,768]{1,0:T(8,128)(2,1)} %collective-permute-done.36.refs_6_), channel_id=1, source_target_pairs={{16,24},{20,28},{17,25},{21,29},{18,26},{22,30},{19,27},{23,31}} | collective-permute-start | bytes 1769480 | tf_op jit(solution)/shard_map/ppermute | solution.py:24
  202.1 43.9 %collective-permute-start.44 = (bf16[512,256]{1,0:T(8,128)(2,1)S(1)}, bf16[512,256]{1,0:T(8,128)(2,1)S(1)}, u32[]{:S(2)}, u32[]{:S(2)}) collective-permute-start(bf16[512,256]{1,0:T(8,128)(2,1)S(1)} %get-tuple-element.21.refs_1_), channel_id=1, source_target_pairs={{0,8},{4,12},{8,16},{12,20},{16,24},{20,28},{1,9},{5,13},{9,17},{1... | collective-permute-start | bytes 786440 | tf_op jit(solution)/shard_map/ppermute | solution.py:24
  243.6 27.6 %collective-permute-start.39 = (bf16[384,768]{1,0:T(8,128)(2,1)}, bf16[384,768]{1,0:T(8,128)(2,1)}, u32[]{:S(2)}, u32[]{:S(2)}) collective-permute-start(bf16[384,768]{1,0:T(8,128)(2,1)} %collective-permute-done.37.refs_7_), channel_id=1, source_target_pairs={{0,4},{4,0},{8,12},{12,8},{1,5},{5,1},{9,13},{13,9},{2,6},{6,2},{1... | collective-permute-start | bytes 1769480 | tf_op jit(solution)/shard_map/ppermute | solution.py:24
  248.8 45.9 %collective-permute-start.43 = (bf16[384,768]{1,0:T(8,128)(2,1)}, bf16[384,768]{1,0:T(8,128)(2,1)S(1)}, u32[]{:S(2)}, u32[]{:S(2)}) collective-permute-start(bf16[384,768]{1,0:T(8,128)(2,1)} %copy-done.8), channel_id=1, source_target_pairs={{0,4},{4,0},{1,5},{5,1},{2,6},{6,2},{3,7},{7,3}} | collective-permute-start | bytes 1769480 | tf_op jit(solution)/shard_map/ppermute | solution.py:24
  253.3 41.5 %collective-permute-start.38 = (bf16[384,768]{1,0:T(8,128)(2,1)}, bf16[384,768]{1,0:T(8,128)(2,1)S(1)}, u32[]{:S(2)}, u32[]{:S(2)}) collective-permute-start(bf16[384,768]{1,0:T(8,128)(2,1)} %collective-permute-done.36.refs_6_), channel_id=1, source_target_pairs={{16,20},{20,16},{24,28},{28,24},{17,21},{21,17},{25,29},{29,25},{1... | collective-permute-start | bytes 1769480 | tf_op jit(solution)/shard_map/ppermute | solution.py:24
  254.0 40.8 %collective-permute-start.42 = (bf16[384,768]{1,0:T(8,128)(2,1)}, bf16[384,768]{1,0:T(8,128)(2,1)S(1)}, u32[]{:S(2)}, u32[]{:S(2)}) collective-permute-start(bf16[384,768]{1,0:T(8,128)(2,1)} %collective-permute-done.40.refs_10_), channel_id=1, source_target_pairs={{24,28},{28,24},{25,29},{29,25},{26,30},{30,26},{27,31},{31,27}} | collective-permute-start | bytes 1769480 | tf_op jit(solution)/shard_map/ppermute | solution.py:24
  258.5 30.8 %collective-permute-start.45 = (bf16[512,256]{1,0:T(8,128)(2,1)S(1)}, bf16[512,256]{1,0:T(8,128)(2,1)S(1)}, u32[]{:S(2)}, u32[]{:S(2)}) collective-permute-start(bf16[512,256]{1,0:T(8,128)(2,1)S(1)} %broadcast_select_fusion.2), channel_id=1, source_target_pairs={{0,4},{4,0},{8,12},{12,8},{16,20},{20,16},{24,28},{28,24},{1,5},{5... | collective-permute-start | bytes 786440 | tf_op jit(solution)/shard_map/ppermute | solution.py:24
  (42 other events, 936.1 us)
where the time goes:
time: 318 us; the launch traced here: 317 us
  waiting for transfers between devices  157 us (49%)
  starting transfers between devices  98 us (31%)
  Pallas kernels  48.6 us (15%)
  local copies, waits for them, and re-layouts  10.5 us (3%)
    ppermute x49, waiting for transfers between devices, moved(): return lax.ppermute(block, axis, route)  149 us
    ppermute x49, starting transfers between devices, moved(): return lax.ppermute(block, axis, route)  97.5 us
    pallas_call x4, Pallas kernels, attend(): pl.pallas_call(functools.partial(attend_kernel, arrays=arrays, groups=tup...  32.4 us
    ppermute x1, waiting for transfers between devices, paired_layer(): corner = lax.ppermute(o_theirs, ('seq', 'head'), route)  7.62 us
  transfers between devices with their start and end apart: 50, of which 16 were waited for; matrix products, arithmetic and copies ran while one was open for 2% of the time, Pallas kernels for 13%

commit v1 on v0

--- a/solution.py
+++ b/solution.py
@@ -14,6 +14,7 @@
 EPSILON = 1e-06
 SELF_TILE = 256
 VMEM_LIMIT = 24 * 2**20
+PROJECT_LIMIT = 32 * 2**20
 CROSS_TILE = 256
 LOG2E = 1.4426950408889634
 
@@ -245,140 +246,128 @@
     )(places, base, *pieces, *w_blocks)
 
 
-def norm_into(lane, gain_ref, hidden_refs, normed_ref):
-    wide = hidden_refs[0].shape[1]
+def norm_into(lane, gain_ref, pieces, at_row, normed_ref):
+    wide = pieces[0][0].shape[1]
+    rows = pieces[0][1].stop - pieces[0][1].start
     total = 0.0
-    for ref in hidden_refs:
-        x = ref[...].astype(jnp.float32)
+    for ref, part in pieces:
+        x = ref[part, :].astype(jnp.float32)
         total += jnp.sum(x * x, axis=1, keepdims=True)
-    scale = lax.rsqrt(total / (wide * len(hidden_refs)) + EPSILON)
-    for step, ref in enumerate(hidden_refs):
+    scale = lax.rsqrt(total / (wide * len(pieces)) + EPSILON)
+    for step, (ref, part) in enumerate(pieces):
         at = pl.multiple_of((lane ^ step) * wide, wide)
-        x = ref[...].astype(jnp.float32)
-        normed_ref[:, pl.ds(at, wide)] = (x * scale * gain_ref[:, pl.ds(at, wide)]).astype(
+        x = ref[part, :].astype(jnp.float32)
+        normed_ref[at_row : at_row + rows, pl.ds(at, wide)] = (
+            x * scale * gain_ref[:, pl.ds(at, wide)]
+        ).astype(jnp.bfloat16)
+
+
+def fetch(place_ref, pieces, buffer, sems, rings):
+    z = place_ref[0] // 2
+    for k in range(rings):
+
+        def begin(name, k=k):
+            pltpu.make_async_copy(pieces[name], buffer.at[k], sems.at[k]).start()
+
+        if k == 0:
+            begin(("w", 0))
+        else:
+
+            @pl.when(z >= k)
+            def _(k=k, begin=begin):
+                begin(("up", k))
+
+            @pl.when(z < k)
+            def _(k=k, begin=begin):
+                begin(("down", rings - k))
+
+
+def gather_dot(place_ref, normed, pieces, buffer, sems, rings):
+    z = place_ref[0] // 2
+    depth = buffer.shape[1]
+    total = 0.0
+    for k in range(rings):
+        if sems is not None:
+            pltpu.make_async_copy(pieces[("w", 0)], buffer.at[k], sems.at[k]).wait()
+        at = pl.multiple_of(lax.rem(z - k + rings, rings) * depth, depth)
+        total += jnp.dot(normed[:, pl.ds(at, depth)], buffer[k], preferred_element_type=jnp.float32)
+    return total
+
+
+def cache_call(place1, lane1, gain, hiddens, pieces, rings):
+    names = list(pieces)
+    depth, width = pieces[("w", 0)].shape
+    arrays = [a for _, group in hiddens for a, _ in group]
+    total = sum(part.stop - part.start for _, ((_, part), *_) in hiddens)
+    wide = arrays[0].shape[1] * len(hiddens[0][1])
+
+    def kernel(place_ref, lane_ref, gain_ref, *refs):
+        hidden_refs = refs[: len(arrays)]
+        piece_refs = refs[len(arrays) : len(arrays) + len(names)]
+        normed_ref, cache_ref, buffer, sems = refs[len(arrays) + len(names) :]
+        at = dict(zip(names, piece_refs))
+        fetch(place_ref, at, buffer, sems, rings)
+        taken = 0
+        for row, group in hiddens:
+            pairs = [(hidden_refs[taken + n], part) for n, (_, part) in enumerate(group)]
+            taken += len(group)
+            norm_into(lane_ref[0], gain_ref, pairs, row, normed_ref)
+        cache_ref[...] = gather_dot(place_ref, normed_ref, at, buffer, sems, rings).astype(
             jnp.bfloat16
         )
-
-
-def fetch(place_ref, pieces, columns, buffer, sems, rings):
-    z, y = place_ref[0] // 2, lax.rem(place_ref[0], 2)
-    depth = buffer.shape[1] // 2
-    order = []
-    for k in range(rings):
-        order.append(lax.rem(z - k + rings, rings))
-        for t in (0, 1):
-            rows = pl.ds(pl.multiple_of((y ^ t) * depth, depth), depth)
-
-            def begin(name, slot=2 * k + t, k=k, rows=rows):
-                ref, base = pieces[name]
-                pltpu.make_async_copy(
-                    ref.at[:, columns.start - base : columns.stop - base],
-                    buffer.at[k, rows],
-                    sems.at[slot],
-                ).start()
-
-            if k == 0:
-                begin(("w", 0, t))
-            else:
-
-                @pl.when(z >= k)
-                def _(k=k, t=t, begin=begin):
-                    begin(("up", k, t))
-
-                @pl.when(z < k)
-                def _(k=k, t=t, begin=begin):
-                    begin(("down", rings - k, t))
-
-    return order
-
-
-def gather_dot(normed_ref, order, pieces, columns, buffer, sems):
-    total = 0.0
-    first = pieces[("w", 0, 0)][0]
-    depth = first.shape[0]
-    for k, block in enumerate(order):
-        for t in (0, 1):
-            pltpu.make_async_copy(
-                first.at[:, 0 : columns.stop - columns.start],
-                buffer.at[k, pl.ds(t * depth, depth)],
-                sems.at[2 * k + t],
-            ).wait()
-        at = pl.multiple_of(block * 2 * depth, 2 * depth)
-        total += jnp.dot(
-            normed_ref[:, pl.ds(at, 2 * depth)], buffer[k], preferred_element_type=jnp.float32
-        )
-    return total
-
-
-def cache_call(place1, lane1, gain, hiddens, pieces, width, rings):
-    names = list(pieces)
-    rows, own = hiddens[0].shape
-    depth = pieces[("w", 0, 0)][0].shape[0]
-    groups = width // (2 * HEAD_DIM)
-    columns = slice(0, width)
-
-    def kernel(place_ref, lane_ref, gain_ref, *refs):
-        hidden_refs = refs[: len(hiddens)]
-        piece_refs = refs[len(hiddens) : len(hiddens) + len(names)]
-        normed_ref, *cache_refs = refs[len(hiddens) + len(names) : -2]
-        buffer, sems = refs[-2:]
-        at = {n: (r, pieces[n][1]) for n, r in zip(names, piece_refs)}
-        order = fetch(place_ref, at, columns, buffer, sems, rings)
-        norm_into(lane_ref[0], gain_ref, hidden_refs, normed_ref)
-        total = gather_dot(normed_ref, order, at, columns, buffer, sems)
-        for g, ref in enumerate(cache_refs):
-            for part in (0, 1):
-                c = (part * groups + g) * HEAD_DIM
-                ref[:, part * HEAD_DIM : (part + 1) * HEAD_DIM] = total[
-                    :, c : c + HEAD_DIM
-                ].astype(jnp.bfloat16)
 
     vmem = pl.BlockSpec(memory_space=pltpu.VMEM)
     smem = pl.BlockSpec(memory_space=pltpu.SMEM)
     return pl.pallas_call(
         kernel,
-        out_shape=[jax.ShapeDtypeStruct((rows, own * len(hiddens)), jnp.bfloat16)]
-        + [jax.ShapeDtypeStruct((rows, 2 * HEAD_DIM), jnp.bfloat16)] * groups,
+        out_shape=[
+            jax.ShapeDtypeStruct((total, wide), jnp.bfloat16),
+            jax.ShapeDtypeStruct((total, width), jnp.bfloat16),
+        ],
         in_specs=[smem, smem, vmem]
-        + [vmem] * len(hiddens)
+        + [vmem] * len(arrays)
         + [pl.BlockSpec(memory_space=pl.ANY)] * len(names),
-        out_specs=[vmem] * (1 + groups),
+        out_specs=[vmem] * 2,
         scratch_shapes=[
-            pltpu.VMEM((rings, 2 * depth, width), jnp.bfloat16),
-            pltpu.SemaphoreType.DMA((2 * rings,)),
+            pltpu.VMEM((rings, depth, width), jnp.bfloat16),
+            pltpu.SemaphoreType.DMA((rings,)),
         ],
-        compiler_params=pltpu.CompilerParams(vmem_limit_bytes=VMEM_LIMIT),
+        compiler_params=pltpu.CompilerParams(vmem_limit_bytes=PROJECT_LIMIT),
         name="cache",
-    )(place1, lane1, gain, *hiddens, *[pieces[n][0] for n in names])
-
-
-def query_call(place1, normed, pieces, start, width, rings):
+    )(place1, lane1, gain, *arrays, *[pieces[n] for n in names])
+
+
+def query_call(place1, normed, pieces, rings):
     names = list(pieces)
-    rows = normed.shape[0]
-    depth = pieces[("w", 0, 0)][0].shape[0]
-    columns = slice(start, start + width)
-
-    def kernel(place_ref, normed_ref, *refs):
-        piece_refs = refs[: len(names)]
-        o_ref, buffer, sems = refs[len(names) :]
-        at = {n: (r, pieces[n][1]) for n, r in zip(names, piece_refs)}
-        order = fetch(place_ref, at, columns, buffer, sems, rings)
-        o_ref[...] = gather_dot(normed_ref, order, at, columns, buffer, sems).astype(jnp.bfloat16)
+    depth, width = pieces[("w", 0)].shape
+    count = len(normed)
+
+    def kernel(place_ref, *refs):
+        normed_refs, refs = refs[:count], refs[count:]
+        piece_refs, refs = refs[: len(names)], refs[len(names) :]
+        o_refs, (buffer, sems) = refs[:count], refs[count:]
+        at = dict(zip(names, piece_refs))
+        fetch(place_ref, at, buffer, sems, rings)
+        for n in range(count):
+            o_refs[n][...] = gather_dot(
+                place_ref, normed_refs[n], at, buffer, None if n else sems, rings
+            ).astype(jnp.bfloat16)
 
     vmem = pl.BlockSpec(memory_space=pltpu.VMEM)
     return pl.pallas_call(
         kernel,
-        out_shape=jax.ShapeDtypeStruct((rows, width), jnp.bfloat16),
-        in_specs=[pl.BlockSpec(memory_space=pltpu.SMEM), vmem]
+        out_shape=[jax.ShapeDtypeStruct((a.shape[0], width), jnp.bfloat16) for a in normed],
+        in_specs=[pl.BlockSpec(memory_space=pltpu.SMEM)]
+        + [vmem] * count
         + [pl.BlockSpec(memory_space=pl.ANY)] * len(names),
-        out_specs=vmem,
+        out_specs=[vmem] * count,
         scratch_shapes=[
-            pltpu.VMEM((rings, 2 * depth, width), jnp.bfloat16),
-            pltpu.SemaphoreType.DMA((2 * rings,)),
+            pltpu.VMEM((rings, depth, width), jnp.bfloat16),
+            pltpu.SemaphoreType.DMA((rings,)),
         ],
-        compiler_params=pltpu.CompilerParams(vmem_limit_bytes=VMEM_LIMIT),
+        compiler_params=pltpu.CompilerParams(vmem_limit_bytes=PROJECT_LIMIT),
         name="queries",
-    )(place1, normed, *[pieces[n][0] for n in names])
+    )(place1, *normed, *[pieces[n] for n in names])
 
 
 def paired_layer(
@@ -396,11 +385,10 @@
     seq,
     head,
 ):
-    _, own = residual.shape
+    rows, own = residual.shape
     half = own // 2
     parts = half // HEAD_DIM
     rings = seq // 2
-    groups = w_cache.shape[1] // (2 * HEAD_DIM)
     place = lax.axis_index("seq").astype(jnp.int32)
     lane = lax.axis_index("head").astype(jnp.int32)
     side = lax.rem(place, 2)
@@ -413,6 +401,7 @@
         )
 
     up = lambda i: i + 2
+    down = lambda i: i - 2
     swap = lambda i: i ^ 1
     column = lambda a, at, size: lax.dynamic_slice_in_dim(a, at, size, 1)
 
@@ -437,25 +426,38 @@
         piece = lax.dynamic_slice_in_dim(source, (lane ^ step) * own, own, 1)
         w_blocks.append(send(piece, "head", lambda i: i ^ step))
 
-    wide = w_cache.shape[1]
+    kv_width = w_cache.shape[1] // 2
+    kv_half = kv_width // 2
+
+    def columns_of(which):
+        return jnp.concatenate(
+            [
+                column(w_cache, which * kv_half, kv_half),
+                column(w_cache, kv_width + which * kv_half, kv_half),
+                column(w_query, which * half, half),
+            ],
+            axis=1,
+        )
+
+    def ordered(kept, got, axis):
+        return jnp.where(
+            side == 0,
+            jnp.concatenate([kept, got], axis=axis),
+            jnp.concatenate([got, kept], axis=axis),
+        )
+
+    w_kept = columns_of(side)
+    w_got = send(columns_of(1 - side), "seq", swap)
     tables = []
-    for name, w, base in (("c", w_cache, 0), ("q", w_query, wide)):
-        table = {("w", 0, 0): (w, base)}
-        table[("w", 0, 1)] = (send(w, "seq", swap), base)
-        high = w
+    for start, stop in ((0, kv_width), (kv_width, kv_width + half)):
+        w = ordered(w_kept[:, start:stop], w_got[:, start:stop], 0)
+        table = {("w", 0): w}
+        high = low = w
         for k in range(1, rings):
-            if name == "q":
-                high = send(high, "seq", up, lambda i: i // 2 >= k - 1)
-            else:
-                rises = lambda i: i // 2 + k < rings
-                high = send(w, "seq", lambda i: i + 2 * k, rises)
-            low = send(w, "seq", lambda i: i - 2 * k, lambda i: i // 2 >= k)
-            table[("up", k, 0)] = (high, base)
-            table[("down", k, 0)] = (low, base)
-            risen = lambda i: i // 2 >= k
-            fallen = lambda i: i // 2 < rings - k
-            table[("up", k, 1)] = (send(high, "seq", swap, risen), base)
-            table[("down", k, 1)] = (send(low, "seq", swap, fallen), base)
+            high = send(high, "seq", up, lambda i: i // 2 >= k - 1)
+            low = send(low, "seq", down, lambda i: i // 2 <= rings - k)
+            table[("up", k)] = high
+            table[("down", k)] = low
         tables.append(table)
     cache_pieces, query_pieces = tables
 
@@ -505,49 +507,65 @@
         False,
         jnp.bfloat16,
     )
-    hidden_x = send(hidden, "head", lambda i: i ^ 2)
-    hidden_c = send(hidden, "head", lambda i: i ^ 1)
-    hidden_xc = send(hidden_x, "head", lambda i: i ^ 1)
-    normed, *caches = cache_call(
-        place1,
-        lane1,
-        norm_gain[None, :],
-        [hidden, hidden_c, hidden_x, hidden_xc],
-        cache_pieces,
-        wide,
-        rings,
-    )
-    history = []
-    for cache in caches:
-        two = send(cache, "seq", up)
-        chosen = jnp.where(side == 0, cache, two)
-        one = send(chosen, "seq", swap)
-        three = send(one, "seq", up)
-        history.append([cache, two, one, three])
-    cross_queries = query_call(place1, normed, query_pieces, wide, w_query.shape[1], rings)
-    per = own // HEAD_DIM // groups
-    shape = [(per, True)] * groups
-    begun, *state = attend(
+    cut = rows // 2
+    beside = lambda i: i ^ 2
+    hidden_x = send(hidden, "head", beside)
+    hidden_y = send(hidden, "seq", swap)
+    corner_a = send(hidden_x[:cut], "seq", swap)
+    corner_b = send(hidden_y[cut:], "head", beside)
+    core = {}
+    for name, piece in (
+        ("hc", hidden),
+        ("hxc", hidden_x),
+        ("hyc", hidden_y),
+        ("hxyac", corner_a),
+        ("hxybc", corner_b),
+    ):
+        core[name] = send(piece, "head", flip)
+    every, low_rows, high_rows = slice(0, rows), slice(0, cut), slice(cut, rows)
+    gain = norm_gain[None, :]
+    group = [(0, [(a, every) for a in (hidden, core["hc"], hidden_x, core["hxc"])])]
+    normed_mine, cache_mine = cache_call(place1, lane1, gain, group, cache_pieces, rings)
+    groups = [
+        (
+            0,
+            [(hidden_y, low_rows), (core["hyc"], low_rows)]
+            + [(a, low_rows) for a in (corner_a, core["hxyac"])],
+        ),
+        (
+            cut,
+            [(hidden_y, high_rows), (core["hyc"], high_rows)]
+            + [(a, low_rows) for a in (corner_b, core["hxybc"])],
+        ),
+    ]
+    normed_near, cache_near = cache_call(place1, lane1, gain, groups, cache_pieces, rings)
+    q_pair = query_call(place1, [normed_mine, normed_near], query_pieces, rings)
+    cache_above = send(cache_mine, "seq", up)
+    cache_across = send(cache_near, "seq", up)
+    cache_odd = jnp.where(side == 1, cache_above, cache_across)
+    cache_far = send(cache_odd, "seq", up, lambda i: i >= 2)
+    o_mine, o_theirs, *state = attend(
         scalars,
-        [cross_queries],
-        [slot for blocks in history for slot in blocks[:3]],
-        shape,
-        [("back", 0), ("back", 2), ("back", 1)],
-        [("back", 0)],
+        q_pair,
+        [cache_mine, cache_near, cache_above, cache_across],
+        [(parts, True)],
+        pair + [("back", 2), ("pair", 2)],
+        pair,
         CROSS_TILE,
         "begin",
     )
-    (cross_context,) = attend(
+    o_mine, o_theirs = attend(
         scalars,
-        [cross_queries],
-        [blocks[3] for blocks in history],
-        shape,
-        [("back", 3)],
-        [("back", 0)],
+        q_pair,
+        [cache_far],
+        [(parts, True)],
+        [("odd", 2)],
+        pair,
         CROSS_TILE,
         "finish",
-        [*state, begun],
-    )
+        [*state, o_mine, o_theirs],
+    )
+    cross_context = ordered(o_mine, send(o_theirs, "seq", swap), 1)
     return (hidden, cross_context)
 
 

time: 318 us -> 235 us (0.74)
  starting transfers between devices: 98 us -> 49.7 us
  waiting for transfers between devices: 157 us -> 116 us
  local copies, waits for them, and re-layouts: 10.5 us -> 13.9 us
    ppermute x49 -> x40, starting transfers between devices: 97.5 us -> 48.2 us  [moved(): return lax.ppermute(block, axis, route)]
    ppermute x49 -> x40, waiting for transfers between devices: 149 us -> 108 us  [moved(): return lax.ppermute(block, axis, route)]
    pallas_call x4, Pallas kernels: 32.4 us -> 28.9 us  [attend(): pl.pallas_call(functools.partial(attend_kernel, arrays=arrays, groups=tup...]
    pallas_call x2 -> x3, Pallas kernels: 10 us -> 13.3 us  [the longest x2 8.93 us: cache_call(): pl.pallas_call(kernel, out_shape=[jax.ShapeDtypeStruct((total, wide), jnp...]
  transfers between devices with their start and end apart: 50 -> 41, of which waited for: 16 -> 14; matrix products, arithmetic and copies ran while one was open for 2% -> 5% of each run, Pallas kernels for 13% -> 20%
where the time goes in v1:
time: 235 us; the launch traced here: 234 us
  waiting for transfers between devices  116 us (49%)
  Pallas kernels  50.2 us (21%)
  starting transfers between devices  49.7 us (21%)
  local copies, waits for them, and re-layouts  13.9 us (6%)
  other arithmetic  3.71 us (2%)
    ppermute x40, waiting for transfers between devices, moved(): return lax.ppermute(block, axis, route)  108 us
    ppermute x40, starting transfers between devices, moved(): return lax.ppermute(block, axis, route)  48.2 us
    pallas_call x4, Pallas kernels, attend(): pl.pallas_call(functools.partial(attend_kernel, arrays=arrays, groups=tup...  28.9 us
    pallas_call x2, Pallas kernels, cache_call(): pl.pallas_call(kernel, out_shape=[jax.ShapeDtypeStruct((total, wide), jnp...  8.93 us
    ppermute x1, waiting for transfers between devices, paired_layer(): corner = lax.ppermute(o_theirs, ('seq', 'head'), route)  7.94 us
    pallas_call x2, Pallas kernels, project_call(): pl.pallas_call(kernel, grid_spec=pltpu.PrefetchScalarGridSpec(num_scalar_...  7.91 us
    dynamic_slice x2, local copies, waits for them, and re-layouts, paired_layer(): piece = lax.dynamic_slice_in_dim(source, (lane ^ step) * own, own, 1)  5.55 us
    dynamic_slice x4, local copies, waits for them, and re-layouts, paired_layer(): column = lambda a, at, size: lax.dynamic_slice_in_dim(a, at, size, 1)  4.91 us
  transfers between devices with their start and end apart: 41, of which 14 were waited for; matrix products, arithmetic and copies ran while one was open for 5% of the time, Pallas kernels for 20%

profile of v1, /device:TPU:0, one launch (start us, length us, event | category | flops | bytes accessed | tf_op | source)
XLA Modules:
  0.0 234.5 jit_solution(15263414731346192819)
XLA Ops:
  5.4 3.5 %collective-permute-start.1 = (bf16[512,768]{1,0:T(8,128)(2,1)S(1)}, bf16[512,768]{1,0:T(8,128)(2,1)S(1)}, u32[]{:S(2)}, u32[]{:S(2)}) collective-permute-start(bf16[512,768]{1,0:T(8,128)(2,1)S(1)} %pad_maximum_fusion.refs_2_), channel_id=1, source_target_pairs={{0,8},{4,12},{8,16},{12,20},{16,24},{20,28},{1,9},{5,13},{9,17},{1... | collective-permute-start | bytes 2359304 | tf_op jit(solution)/shard_map/ppermute | solution.py:25
  8.9 14.0 %collective-permute-done.2.refs_3_ = bf16[512,768]{1,0:T(8,128)(2,1)} collective-permute-done((bf16[512,768]{1,0:T(8,128)(2,1)S(1)}, bf16[512,768]{1,0:T(8,128)(2,1)}, u32[]{:S(2)}, u32[]{:S(2)}) %collective-permute-start.2) | collective-permute-done | bytes 786464 | tf_op jit(solution)/shard_map/ppermute | solution.py:25
  23.0 3.7 %collective-permute-start.3 = (bf16[512,768]{1,0:T(8,128)(2,1)}, bf16[512,768]{1,0:T(8,128)(2,1)S(1)}, u32[]{:S(2)}, u32[]{:S(2)}) collective-permute-start(bf16[512,768]{1,0:T(8,128)(2,1)} %collective-permute-done.2.refs_3_), channel_id=1, source_target_pairs={{0,8},{4,12},{8,16},{12,20},{16,24},{20,28},{1,9},{5,13},{9,17},{1... | collective-permute-start | bytes 2359304 | tf_op jit(solution)/shard_map/ppermute | solution.py:25
  36.5 6.4 %collective-permute-done.3.refs_5_ = bf16[512,768]{1,0:T(8,128)(2,1)S(1)} collective-permute-done((bf16[512,768]{1,0:T(8,128)(2,1)}, bf16[512,768]{1,0:T(8,128)(2,1)S(1)}, u32[]{:S(2)}, u32[]{:S(2)}) %collective-permute-start.3) | collective-permute-done | bytes 786464 | tf_op jit(solution)/shard_map/ppermute | solution.py:25
  49.8 11.5 %attend.4 = (bf16[512,384]{1,0:T(8,128)(2,1)S(1)}, bf16[512,384]{1,0:T(8,128)(2,1)S(1)}, f32[512,128]{1,0:T(8,128)S(1)}, f32[512,384]{1,0:T(8,128)S(1)}) custom-call(s32[1]{0:T(128)} %bitcast.place_ref, s32[8]{0:T(128)S(1)} %copy-done.4, s32[8]{0:T(128)S(1)} %copy-done.5, bf16[512,384]{1,0:T(8,128)(2,1)S(1)} %get-tuple-element.45.refs_0_, ...), custom_call_target="tpu_custom_call" | custom-call | tf_op jit(solution)/shard_map/attend/pallas_call | solution.py:191
  61.3 3.5 %attend.5 = (bf16[512,384]{1,0:T(8,128)(2,1)S(1)}, bf16[512,384]{1,0:T(8,128)(2,1)S(1)}) custom-call(s32[1]{0:T(128)} %bitcast.place_ref, s32[8]{0:T(128)S(1)} %copy-done.4, s32[8]{0:T(128)S(1)} %copy-done.5, bf16[512,384]{1,0:T(8,128)(2,1)S(1)} %get-tuple-element.45.refs_0_, bf16[512,384]{1,0:T(8,128)(2,1)S(1)} %collective-permute-done.refs_1_, ...), custom_call_target="tpu_custom_call" | custom-call | tf_op jit(solution)/shard_map/attend/pallas_call | solution.py:191
  68.5 5.4 %collective-permute-done.5.refs_1_ = bf16[512,384]{1,0:T(8,128)(2,1)S(1)} collective-permute-done((bf16[512,384]{1,0:T(8,128)(2,1)S(1)}, bf16[512,384]{1,0:T(8,128)(2,1)S(1)}, u32[]{:S(2)}, u32[]{:S(2)}) %collective-permute-start.5) | collective-permute-done | bytes 393248 | tf_op jit(solution)/shard_map/ppermute | solution.py:25
  73.8 23.6 %collective-permute-done.9.refs_0_ = bf16[512,384]{1,0:T(8,128)(2,1)S(1)} collective-permute-done((bf16[512,384]{1,0:T(8,128)(2,1)S(1)}, bf16[512,384]{1,0:T(8,128)(2,1)S(1)}, u32[]{:S(2)}, u32[]{:S(2)}) %collective-permute-start.9) | collective-permute-done | bytes 393248 | tf_op jit(solution)/shard_map/ppermute | solution.py:25
  97.4 7.9 %collective-permute-done.10.refs_1_ = bf16[512,384]{1,0:T(8,128)(2,1)S(1)} collective-permute-done((bf16[512,384]{1,0:T(8,128)(2,1)S(1)}, bf16[512,384]{1,0:T(8,128)(2,1)S(1)}, u32[]{:S(2)}, u32[]{:S(2)}) %collective-permute-start.10) | collective-permute-done | bytes 393248 | tf_op jit(solution)/shard_map/ppermute | solution.py:489
  107.6 3.5 %collective-permute-start.31 = (bf16[768,384]{1,0:T(8,128)(2,1)S(1)}, bf16[768,384]{1,0:T(8,128)(2,1)S(1)}, u32[]{:S(2)}, u32[]{:S(2)}) collective-permute-start(bf16[768,384]{1,0:T(8,128)(2,1)S(1)} %maximum_select_fusion.1.refs_2_), channel_id=1, source_target_pairs={{0,8},{4,12},{8,16},{12,20},{16,24},{20,28},{1,9},{5,13},{9,17},{1... | collective-permute-start | bytes 1769480 | tf_op jit(solution)/shard_map/ppermute | solution.py:25
  111.3 3.5 %collective-permute-start.19 = (bf16[768,256]{1,0:T(8,128)(2,1)S(1)}, bf16[768,256]{1,0:T(8,128)(2,1)S(1)}, u32[]{:S(2)}, u32[]{:S(2)}) collective-permute-start(bf16[768,256]{1,0:T(8,128)(2,1)S(1)} %maximum_select_fusion.2.refs_4_.refs_8_), channel_id=1, source_target_pairs={{0,8},{4,12},{8,16},{12,20},{16,24},{20,28},{1,9},{5,13},{9,17},{1... | collective-permute-start | bytes 1179656 | tf_op jit(solution)/shard_map/ppermute | solution.py:25
  122.0 4.6 %project.3.refs_0_ = bf16[512,768]{1,0:T(8,128)(2,1)} custom-call(s32[2]{0:T(128)S(1)} %pad_add_fusion.places_ref, f32[512,768]{1,0:T(8,128)S(1)} %project.2.base_ref, bf16[512,384]{1,0:T(8,128)(2,1)S(1)} %collective-permute-done.9.refs_0_, bf16[512,384]{1,0:T(8,128)(2,1)S(1)} %collective-permute-done.10.refs_1_, ...), custom_call_target="tpu_custom_call" | custom-call | tf_op jit(solution)/shard_map/project/pallas_call | solution.py:232
  129.4 3.3 %collective-permute-done.19.refs_5_.refs_9_ = bf16[768,256]{1,0:T(8,128)(2,1)S(1)} collective-permute-done((bf16[768,256]{1,0:T(8,128)(2,1)S(1)}, bf16[768,256]{1,0:T(8,128)(2,1)S(1)}, u32[]{:S(2)}, u32[]{:S(2)}) %collective-permute-start.19) | collective-permute-done | bytes 393248 | tf_op jit(solution)/shard_map/ppermute | solution.py:25
  136.2 10.6 %collective-permute-done.32.refs_4_ = bf16[768,384]{1,0:T(8,128)(2,1)S(1)} collective-permute-done((bf16[768,384]{1,0:T(8,128)(2,1)S(1)}, bf16[768,384]{1,0:T(8,128)(2,1)S(1)}, u32[]{:S(2)}, u32[]{:S(2)}) %collective-permute-start.32) | collective-permute-done | bytes 589856 | tf_op jit(solution)/shard_map/ppermute | solution.py:25
  147.6 6.4 %collective-permute-done.22.refs_8_.refs_12_ = bf16[768,256]{1,0:T(8,128)(2,1)S(1)} collective-permute-done((bf16[768,256]{1,0:T(8,128)(2,1)S(1)}, bf16[768,256]{1,0:T(8,128)(2,1)S(1)}, u32[]{:S(2)}, u32[]{:S(2)}) %collective-permute-start.22) | collective-permute-done | bytes 393248 | tf_op jit(solution)/shard_map/ppermute | solution.py:25
  157.3 8.4 %collective-permute-done.24.refs_10_.refs_14_ = bf16[768,256]{1,0:T(8,128)(2,1)S(1)} collective-permute-done((bf16[768,256]{1,0:T(8,128)(2,1)S(1)}, bf16[768,256]{1,0:T(8,128)(2,1)S(1)}, u32[]{:S(2)}, u32[]{:S(2)}) %collective-permute-start.24) | collective-permute-done | bytes 393248 | tf_op jit(solution)/shard_map/ppermute | solution.py:25
  168.3 6.4 %collective-permute-done.29.refs_6_ = bf16[256,768]{1,0:T(8,128)(2,1)S(1)} collective-permute-done((bf16[256,768]{1,0:T(8,128)(2,1)S(1)}, bf16[256,768]{1,0:T(8,128)(2,1)S(1)}, u32[]{:S(2)}, u32[]{:S(2)}) %collective-permute-start.29) | collective-permute-done | bytes 393248 | tf_op jit(solution)/shard_map/ppermute | solution.py:25
  175.1 4.5 %cache.2 = (bf16[512,3072]{1,0:T(8,128)(2,1)S(1)}, bf16[512,256]{1,0:T(8,128)(2,1)S(1)}) custom-call(s32[1]{0:T(128)} %bitcast.place_ref, s32[1]{0:T(128)} %bitcast.1.lane_ref, f32[1,3072]{1,0:T(1,128)S(1)} %bitcast.3, bf16[512,768]{1,0:T(8,128)(2,1)S(1)} %copy-done.1, bf16[512,768]{1,0:T(8,128)(2,1)S(1)} %collective-permute-done.15.refs_1_, ...), custom_call_target="tpu_custom_call" | custom-call | tf_op jit(solution)/shard_map/cache/pallas_call | solution.py:321
  181.1 4.5 %cache.3 = (bf16[512,3072]{1,0:T(8,128)(2,1)S(1)}, bf16[512,256]{1,0:T(8,128)(2,1)S(1)}) custom-call(s32[1]{0:T(128)} %bitcast.place_ref, s32[1]{0:T(128)} %bitcast.1.lane_ref, f32[1,3072]{1,0:T(1,128)S(1)} %bitcast.4, bf16[512,768]{1,0:T(8,128)(2,1)S(1)} %collective-permute-done.25.refs_0_.refs_4_, ...), custom_call_target="tpu_custom_call" | custom-call | tf_op jit(solution)/shard_map/cache/pallas_call | solution.py:321
  189.6 3.7 %collective-permute-done.38.refs_5_ = bf16[512,256]{1,0:T(8,128)(2,1)S(1)} collective-permute-done((bf16[512,256]{1,0:T(8,128)(2,1)S(1)}, bf16[512,256]{1,0:T(8,128)(2,1)S(1)}, u32[]{:S(2)}, u32[]{:S(2)}) %collective-permute-start.38) | collective-permute-done | bytes 262176 | tf_op jit(solution)/shard_map/ppermute | solution.py:25
  194.0 11.2 %collective-permute-done.36.refs_8_ = bf16[768,384]{1,0:T(8,128)(2,1)S(1)} collective-permute-done((bf16[768,384]{1,0:T(8,128)(2,1)S(1)}, bf16[768,384]{1,0:T(8,128)(2,1)S(1)}, u32[]{:S(2)}, u32[]{:S(2)}) %collective-permute-start.36) | collective-permute-done | bytes 589856 | tf_op jit(solution)/shard_map/ppermute | solution.py:25
  205.1 4.4 %queries.1 = (bf16[512,384]{1,0:T(8,128)(2,1)S(1)}, bf16[512,384]{1,0:T(8,128)(2,1)S(1)}) custom-call(s32[1]{0:T(128)} %bitcast.place_ref, bf16[512,3072]{1,0:T(8,128)(2,1)S(1)} %get-tuple-element.26.refs_0_, bf16[512,3072]{1,0:T(8,128)(2,1)S(1)} %get-tuple-element.27.refs_1_, bf16[768,384]{1,0:T(8,128)(2,1)S(1)} %maximum_select_fusion.1.refs_2_, ...), custom_call_target="tpu_custom_call" | custom-call | tf_op jit(solution)/shard_map/queries/pallas_call | solution.py:357
  209.5 11.0 %attend.6 = (bf16[512,384]{1,0:T(8,128)(2,1)S(1)}, bf16[512,384]{1,0:T(8,128)(2,1)S(1)}, f32[512,128]{1,0:T(8,128)S(1)}, f32[512,384]{1,0:T(8,128)S(1)}) custom-call(s32[1]{0:T(128)} %bitcast.place_ref, s32[8]{0:T(128)S(1)} %copy-done.4, s32[8]{0:T(128)S(1)} %copy-done.5, bf16[512,384]{1,0:T(8,128)(2,1)S(1)} %get-tuple-element.28.refs_0_, ...), custom_call_target="tpu_custom_call" | custom-call | tf_op jit(solution)/shard_map/attend/pallas_call | solution.py:191
  225.0 8.4 %collective-permute-done.40 = bf16[512,384]{1,0:T(8,128)(2,1)S(1)} collective-permute-done((bf16[512,384]{1,0:T(8,128)(2,1)S(1)}, bf16[512,384]{1,0:T(8,128)(2,1)S(1)}, u32[]{:S(2)}, u32[]{:S(2)}) %collective-permute-start.40) | collective-permute-done | bytes 393248 | tf_op jit(solution)/shard_map/ppermute | solution.py:25
  (109 shorter events, 59.5 us)
Async XLA Ops:
  2.3 20.7 %collective-permute-start.2 = (bf16[512,768]{1,0:T(8,128)(2,1)S(1)}, bf16[512,768]{1,0:T(8,128)(2,1)}, u32[]{:S(2)}, u32[]{:S(2)}) collective-permute-start(bf16[512,768]{1,0:T(8,128)(2,1)S(1)} %pad_maximum_fusion.1), channel_id=1, source_target_pairs={{0,4},{4,0},{8,12},{12,8},{16,20},{20,16},{24,28},{28,24},{1,5},{5... | collective-permute-start | bytes 2359304 | tf_op jit(solution)/shard_map/ppermute | solution.py:25
  5.4 30.7 %collective-permute-start.1 = (bf16[512,768]{1,0:T(8,128)(2,1)S(1)}, bf16[512,768]{1,0:T(8,128)(2,1)S(1)}, u32[]{:S(2)}, u32[]{:S(2)}) collective-permute-start(bf16[512,768]{1,0:T(8,128)(2,1)S(1)} %pad_maximum_fusion.refs_2_), channel_id=1, source_target_pairs={{0,8},{4,12},{8,16},{12,20},{16,24},{20,28},{1,9},{5,13},{9,17},{1... | collective-permute-start | bytes 2359304 | tf_op jit(solution)/shard_map/ppermute | solution.py:25
  23.0 19.9 %collective-permute-start.3 = (bf16[512,768]{1,0:T(8,128)(2,1)}, bf16[512,768]{1,0:T(8,128)(2,1)S(1)}, u32[]{:S(2)}, u32[]{:S(2)}) collective-permute-start(bf16[512,768]{1,0:T(8,128)(2,1)} %collective-permute-done.2.refs_3_), channel_id=1, source_target_pairs={{0,8},{4,12},{8,16},{12,20},{16,24},{20,28},{1,9},{5,13},{9,17},{1... | collective-permute-start | bytes 2359304 | tf_op jit(solution)/shard_map/ppermute | solution.py:25
  27.6 20.6 %collective-permute-start = (bf16[512,384]{1,0:T(8,128)(2,1)}, bf16[512,384]{1,0:T(8,128)(2,1)S(1)}, u32[]{:S(2)}, u32[]{:S(2)}) collective-permute-start(bf16[512,384]{1,0:T(8,128)(2,1)} %get-tuple-element.44), channel_id=1, source_target_pairs={{0,4},{4,0},{8,12},{12,8},{16,20},{20,16},{24,28},{28,24},{1,5},{5... | collective-permute-start | bytes 1179656 | tf_op jit(solution)/shard_map/ppermute | solution.py:25
  31.5 35.5 %collective-permute-start.8 = (bf16[768,768]{1,0:T(8,128)(2,1)}, bf16[768,768]{1,0:T(8,128)(2,1)}, u32[]{:S(2)}, u32[]{:S(2)}) collective-permute-start(bf16[768,768]{1,0:T(8,128)(2,1)} %constant_dynamic-slice_fusion.8), channel_id=1, source_target_pairs={{0,1},{1,0},{2,3},{3,2},{4,5},{5,4},{6,7},{7,6},{8,9},{9,8},{10,11... | collective-permute-start | bytes 3538952 | tf_op jit(solution)/shard_map/ppermute | solution.py:25
  34.6 33.8 %collective-permute-start.13 = (bf16[768,768]{1,0:T(8,128)(2,1)}, bf16[768,768]{1,0:T(8,128)(2,1)}, u32[]{:S(2)}, u32[]{:S(2)}) collective-permute-start(bf16[768,768]{1,0:T(8,128)(2,1)} %get-tuple-element.39), channel_id=1, source_target_pairs={{0,2},{1,3},{2,0},{3,1},{4,6},{5,7},{6,4},{7,5},{8,10},{9,11},{10,... | collective-permute-start | bytes 3538952 | tf_op jit(solution)/shard_map/ppermute | solution.py:25
  36.1 71.5 %collective-permute-start.14 = (bf16[768,768]{1,0:T(8,128)(2,1)}, bf16[768,768]{1,0:T(8,128)(2,1)}, u32[]{:S(2)}, u32[]{:S(2)}) collective-permute-start(bf16[768,768]{1,0:T(8,128)(2,1)} %get-tuple-element.38), channel_id=1, source_target_pairs={{0,3},{1,2},{2,1},{3,0},{4,7},{5,6},{6,5},{7,4},{8,11},{9,10},{10,... | collective-permute-start | bytes 3538952 | tf_op jit(solution)/shard_map/ppermute | solution.py:25
  65.4 31.9 %collective-permute-start.9 = (bf16[512,384]{1,0:T(8,128)(2,1)S(1)}, bf16[512,384]{1,0:T(8,128)(2,1)S(1)}, u32[]{:S(2)}, u32[]{:S(2)}) collective-permute-start(bf16[512,384]{1,0:T(8,128)(2,1)S(1)} %get-tuple-element.24.refs_0_), channel_id=1, source_target_pairs={{0,2},{1,3},{2,0},{3,1},{4,6},{5,7},{6,4},{7,5},{8,10},{9,11},{10,... | collective-permute-start | bytes 1179656 | tf_op jit(solution)/shard_map/ppermute | solution.py:25
  66.9 38.4 %collective-permute-start.10 = (bf16[512,384]{1,0:T(8,128)(2,1)S(1)}, bf16[512,384]{1,0:T(8,128)(2,1)S(1)}, u32[]{:S(2)}, u32[]{:S(2)}) collective-permute-start(bf16[512,384]{1,0:T(8,128)(2,1)S(1)} %get-tuple-element.25), channel_id=1, source_target_pairs={{0,6},{1,7},{2,4},{3,5},{4,2},{5,3},{6,0},{7,1},{8,14},{9,15},{10,... | collective-permute-start | bytes 1179656 | tf_op jit(solution)/shard_map/ppermute | solution.py:489
  68.5 42.9 %collective-permute-start.6 = (bf16[512,384]{1,0:T(8,128)(2,1)S(1)}, bf16[512,384]{1,0:T(8,128)(2,1)S(1)}, u32[]{:S(2)}, u32[]{:S(2)}) collective-permute-start(bf16[512,384]{1,0:T(8,128)(2,1)S(1)} %get-tuple-element.24.refs_0_), channel_id=1, source_target_pairs={{0,1},{1,0},{2,3},{3,2},{4,5},{5,4},{6,7},{7,6},{8,9},{9,8},{10,11... | collective-permute-start | bytes 1179656 | tf_op jit(solution)/shard_map/ppermute | solution.py:25
  73.8 41.1 %collective-permute-start.7 = (bf16[512,384]{1,0:T(8,128)(2,1)S(1)}, bf16[512,384]{1,0:T(8,128)(2,1)S(1)}, u32[]{:S(2)}, u32[]{:S(2)}) collective-permute-start(bf16[512,384]{1,0:T(8,128)(2,1)S(1)} %collective-permute-done.5.refs_1_), channel_id=1, source_target_pairs={{0,1},{1,0},{2,3},{3,2},{4,5},{5,4},{6,7},{7,6},{8,9},{9,8},{10,11... | collective-permute-start | bytes 1179656 | tf_op jit(solution)/shard_map/ppermute | solution.py:25
  97.4 24.6 %collective-permute-start.11 = (bf16[512,384]{1,0:T(8,128)(2,1)S(1)}, bf16[512,384]{1,0:T(8,128)(2,1)S(1)}, u32[]{:S(2)}, u32[]{:S(2)}) collective-permute-start(bf16[512,384]{1,0:T(8,128)(2,1)S(1)} %collective-permute-done.9.refs_0_), channel_id=1, source_target_pairs={{0,1},{1,0},{2,3},{3,2},{4,5},{5,4},{6,7},{7,6},{8,9},{9,8},{10,11... | collective-permute-start | bytes 1179656 | tf_op jit(solution)/shard_map/ppermute | solution.py:25
  107.6 27.3 %collective-permute-start.31 = (bf16[768,384]{1,0:T(8,128)(2,1)S(1)}, bf16[768,384]{1,0:T(8,128)(2,1)S(1)}, u32[]{:S(2)}, u32[]{:S(2)}) collective-permute-start(bf16[768,384]{1,0:T(8,128)(2,1)S(1)} %maximum_select_fusion.1.refs_2_), channel_id=1, source_target_pairs={{0,8},{4,12},{8,16},{12,20},{16,24},{20,28},{1,9},{5,13},{9,17},{1... | collective-permute-start | bytes 1769480 | tf_op jit(solution)/shard_map/ppermute | solution.py:25
  111.3 21.4 %collective-permute-start.19 = (bf16[768,256]{1,0:T(8,128)(2,1)S(1)}, bf16[768,256]{1,0:T(8,128)(2,1)S(1)}, u32[]{:S(2)}, u32[]{:S(2)}) collective-permute-start(bf16[768,256]{1,0:T(8,128)(2,1)S(1)} %maximum_select_fusion.2.refs_4_.refs_8_), channel_id=1, source_target_pairs={{0,8},{4,12},{8,16},{12,20},{16,24},{20,28},{1,9},{5,13},{9,17},{1... | collective-permute-start | bytes 1179656 | tf_op jit(solution)/shard_map/ppermute | solution.py:25
  114.9 19.3 %collective-permute-start.20 = (bf16[768,256]{1,0:T(8,128)(2,1)S(1)}, bf16[768,256]{1,0:T(8,128)(2,1)S(1)}, u32[]{:S(2)}, u32[]{:S(2)}) collective-permute-start(bf16[768,256]{1,0:T(8,128)(2,1)S(1)} %maximum_select_fusion.2.refs_4_.refs_8_), channel_id=1, source_target_pairs={{8,0},{12,4},{16,8},{20,12},{24,16},{28,20},{9,1},{13,5},{17,9},{2... | collective-permute-start | bytes 1179656 | tf_op jit(solution)/shard_map/ppermute | solution.py:25
  126.7 28.6 %collective-permute-start.16 = (bf16[512,768]{1,0:T(8,128)(2,1)}, bf16[512,768]{1,0:T(8,128)(2,1)S(1)}, u32[]{:S(2)}, u32[]{:S(2)}) collective-permute-start(bf16[512,768]{1,0:T(8,128)(2,1)} %project.3.refs_0_), channel_id=1, source_target_pairs={{0,2},{1,3},{2,0},{3,1},{4,6},{5,7},{6,4},{7,5},{8,10},{9,11},{10,... | collective-permute-start | bytes 2359304 | tf_op jit(solution)/shard_map/ppermute | solution.py:25
  132.7 22.7 %collective-permute-start.25 = (bf16[512,768]{1,0:T(8,128)(2,1)}, bf16[512,768]{1,0:T(8,128)(2,1)S(1)}, u32[]{:S(2)}, u32[]{:S(2)}) collective-permute-start(bf16[512,768]{1,0:T(8,128)(2,1)} %project.3.refs_0_), channel_id=1, source_target_pairs={{0,4},{4,0},{8,12},{12,8},{16,20},{20,16},{24,28},{28,24},{1,5},{5... | collective-permute-start | bytes 2359304 | tf_op jit(solution)/shard_map/ppermute | solution.py:25
  134.9 19.1 %collective-permute-start.22 = (bf16[768,256]{1,0:T(8,128)(2,1)S(1)}, bf16[768,256]{1,0:T(8,128)(2,1)S(1)}, u32[]{:S(2)}, u32[]{:S(2)}) collective-permute-start(bf16[768,256]{1,0:T(8,128)(2,1)S(1)} %collective-permute-done.20.refs_6_.refs_10_), channel_id=1, source_target_pairs={{8,0},{12,4},{16,8},{20,12},{9,1},{13,5},{17,9},{21,13},{10,2},{14... | collective-permute-start | bytes 1179656 | tf_op jit(solution)/shard_map/ppermute | solution.py:25
  146.9 19.3 %collective-permute-start.15 = (bf16[512,768]{1,0:T(8,128)(2,1)}, bf16[512,768]{1,0:T(8,128)(2,1)S(1)}, u32[]{:S(2)}, u32[]{:S(2)}) collective-permute-start(bf16[512,768]{1,0:T(8,128)(2,1)} %project.3.refs_0_), channel_id=1, source_target_pairs={{0,1},{1,0},{2,3},{3,2},{4,5},{5,4},{6,7},{7,6},{8,9},{9,8},{10,11... | collective-permute-start | bytes 2359304 | tf_op jit(solution)/shard_map/ppermute | solution.py:25
  155.3 19.4 %collective-permute-start.17 = (bf16[512,768]{1,0:T(8,128)(2,1)S(1)}, bf16[512,768]{1,0:T(8,128)(2,1)S(1)}, u32[]{:S(2)}, u32[]{:S(2)}) collective-permute-start(bf16[512,768]{1,0:T(8,128)(2,1)S(1)} %collective-permute-done.16.refs_2_), channel_id=1, source_target_pairs={{0,1},{1,0},{2,3},{3,2},{4,5},{5,4},{6,7},{7,6},{8,9},{9,8},{10,11... | collective-permute-start | bytes 2359304 | tf_op jit(solution)/shard_map/ppermute | solution.py:25
  157.0 22.6 %collective-permute-start.26 = (bf16[512,768]{1,0:T(8,128)(2,1)S(1)}, bf16[512,768]{1,0:T(8,128)(2,1)S(1)}, u32[]{:S(2)}, u32[]{:S(2)}) collective-permute-start(bf16[512,768]{1,0:T(8,128)(2,1)S(1)} %collective-permute-done.25.refs_0_.refs_4_), channel_id=1, source_target_pairs={{0,1},{1,0},{2,3},{3,2},{4,5},{5,4},{6,7},{7,6},{8,9},{9,8},{10,11... | collective-permute-start | bytes 2359304 | tf_op jit(solution)/shard_map/ppermute | solution.py:25
  166.2 21.3 %collective-permute-start.33 = (bf16[768,384]{1,0:T(8,128)(2,1)S(1)}, bf16[768,384]{1,0:T(8,128)(2,1)S(1)}, u32[]{:S(2)}, u32[]{:S(2)}) collective-permute-start(bf16[768,384]{1,0:T(8,128)(2,1)S(1)} %collective-permute-done.31.refs_3_), channel_id=1, source_target_pairs={{8,16},{12,20},{16,24},{20,28},{9,17},{13,21},{17,25},{21,29},{10,... | collective-permute-start | bytes 1769480 | tf_op jit(solution)/shard_map/ppermute | solution.py:25
  167.0 21.3 %collective-permute-start.34 = (bf16[768,384]{1,0:T(8,128)(2,1)S(1)}, bf16[768,384]{1,0:T(8,128)(2,1)S(1)}, u32[]{:S(2)}, u32[]{:S(2)}) collective-permute-start(bf16[768,384]{1,0:T(8,128)(2,1)S(1)} %collective-permute-done.32.refs_4_), channel_id=1, source_target_pairs={{8,0},{12,4},{16,8},{20,12},{9,1},{13,5},{17,9},{21,13},{10,2},{14... | collective-permute-start | bytes 1769480 | tf_op jit(solution)/shard_map/ppermute | solution.py:25
  193.3 27.2 %collective-permute-start.39 = (bf16[512,256]{1,0:T(8,128)(2,1)S(1)}, bf16[512,256]{1,0:T(8,128)(2,1)S(1)}, u32[]{:S(2)}, u32[]{:S(2)}) collective-permute-start(bf16[512,256]{1,0:T(8,128)(2,1)S(1)} %broadcast_select_fusion.1), channel_id=1, source_target_pairs={{8,16},{12,20},{16,24},{20,28},{9,17},{13,21},{17,25},{21,29},{10,... | collective-permute-start | bytes 786440 | tf_op jit(solution)/shard_map/ppermute | solution.py:25
  (29 other events, 451.8 us)

commit v2 on v1

--- a/solution.py
+++ b/solution.py
@@ -211,8 +211,9 @@
     half = own // 2
 
     def kernel(places_ref, base_ref, *refs):
-        near_refs, w_refs = refs[: len(pieces)], refs[len(pieces) : -2]
-        o_ref, context_ref = refs[-2:]
+        near_refs, refs = refs[: len(pieces)], refs[len(pieces) :]
+        w_refs, o_refs = refs[: len(w_blocks)], refs[len(w_blocks) : -1]
+        context_ref = refs[-1]
         side = lax.rem(places_ref[0], 2)
         for step, ref in enumerate(near_refs):
             block, other = divmod(step, 2)
@@ -225,8 +226,13 @@
                 w_ref[...],
                 preferred_element_type=jnp.float32,
             )
-        o_ref[...] = total.astype(o_ref.dtype)
-
+        total = total.astype(out_type)
+        o_refs[0][...] = total
+        for n, ref in enumerate(o_refs[1:]):
+            ref[...] = total[n * cut : (n + 1) * cut]
+
+    cut = rows // 2
+    shapes = [base.shape] if first else [base.shape, (cut, own), (cut, own)]
     whole = lambda a: pl.BlockSpec(a.shape, lambda i, places_ref: (0, 0))
     corner = pl.BlockSpec((own, own), lambda i, places_ref: (0, places_ref[1] if first else 0))
     return pl.pallas_call(
@@ -237,10 +243,10 @@
             in_specs=[whole(a) for a in (base, *pieces)]
             + [corner]
             + [whole(w) for w in w_blocks[1:]],
-            out_specs=whole(base),
+            out_specs=[pl.BlockSpec(s, lambda i, places_ref: (0, 0)) for s in shapes],
             scratch_shapes=[pltpu.VMEM((rows, own * len(w_blocks)), jnp.bfloat16)],
         ),
-        out_shape=jax.ShapeDtypeStruct((rows, own), out_type),
+        out_shape=[jax.ShapeDtypeStruct(s, out_type) for s in shapes],
         compiler_params=pltpu.CompilerParams(vmem_limit_bytes=VMEM_LIMIT),
         name="project",
     )(places, base, *pieces, *w_blocks)
@@ -449,13 +455,16 @@
     w_kept = columns_of(side)
     w_got = send(columns_of(1 - side), "seq", swap)
     tables = []
-    for start, stop in ((0, kv_width), (kv_width, kv_width + half)):
+    for name, start, stop in (("c", 0, kv_width), ("q", kv_width, kv_width + half)):
         w = ordered(w_kept[:, start:stop], w_got[:, start:stop], 0)
         table = {("w", 0): w}
         high = low = w
         for k in range(1, rings):
             high = send(high, "seq", up, lambda i: i // 2 >= k - 1)
-            low = send(low, "seq", down, lambda i: i // 2 <= rings - k)
+            if name == "c" or k == rings - 1:
+                low = send(w, "seq", lambda i: i - 2 * k)
+            else:
+                low = send(low, "seq", down, lambda i: i // 2 <= rings - k)
             table[("up", k)] = high
             table[("down", k)] = low
         tables.append(table)
@@ -491,7 +500,7 @@
     places = jnp.stack([place, lane])
     contexts = [o_mine, send(o_theirs, "seq", swap), send(o_mine, "head", lambda i: i ^ 2), corner]
     others = [send(piece, "head", flip) for piece in contexts]
-    partial = project_call(
+    (partial,) = project_call(
         places,
         residual,
         contexts[:2] + others[:2],
@@ -499,7 +508,7 @@
         True,
         jnp.float32,
     )
-    hidden = project_call(
+    hidden, hidden_low, hidden_high = project_call(
         places,
         partial,
         contexts[2:] + others[2:],
@@ -507,36 +516,29 @@
         False,
         jnp.bfloat16,
     )
+    beside = lambda i: i ^ 2
+    x_low = send(hidden_low, "head", beside)
+    y_high = send(hidden_high, "seq", swap)
+    x_high = send(hidden_high, "head", beside)
+    y_low = send(hidden_low, "seq", swap)
+    corner_low = send(x_low, "seq", swap)
+    corner_high = send(y_high, "head", beside)
+    own_core = send(hidden, "head", flip)
+    core = [
+        send(piece, "head", flip)
+        for piece in (x_low, x_high, y_low, y_high, corner_low, corner_high)
+    ]
     cut = rows // 2
-    beside = lambda i: i ^ 2
-    hidden_x = send(hidden, "head", beside)
-    hidden_y = send(hidden, "seq", swap)
-    corner_a = send(hidden_x[:cut], "seq", swap)
-    corner_b = send(hidden_y[cut:], "head", beside)
-    core = {}
-    for name, piece in (
-        ("hc", hidden),
-        ("hxc", hidden_x),
-        ("hyc", hidden_y),
-        ("hxyac", corner_a),
-        ("hxybc", corner_b),
-    ):
-        core[name] = send(piece, "head", flip)
-    every, low_rows, high_rows = slice(0, rows), slice(0, cut), slice(cut, rows)
+    whole, low_rows, high_rows = slice(0, cut), slice(0, cut), slice(cut, rows)
     gain = norm_gain[None, :]
-    group = [(0, [(a, every) for a in (hidden, core["hc"], hidden_x, core["hxc"])])]
-    normed_mine, cache_mine = cache_call(place1, lane1, gain, group, cache_pieces, rings)
     groups = [
-        (
-            0,
-            [(hidden_y, low_rows), (core["hyc"], low_rows)]
-            + [(a, low_rows) for a in (corner_a, core["hxyac"])],
-        ),
-        (
-            cut,
-            [(hidden_y, high_rows), (core["hyc"], high_rows)]
-            + [(a, low_rows) for a in (corner_b, core["hxybc"])],
-        ),
+        (0, [(hidden, low_rows), (own_core, low_rows), (x_low, whole), (core[0], whole)]),
+        (cut, [(hidden, high_rows), (own_core, high_rows), (x_high, whole), (core[1], whole)]),
+    ]
+    normed_mine, cache_mine = cache_call(place1, lane1, gain, groups, cache_pieces, rings)
+    groups = [
+        (0, [(a, whole) for a in (y_low, core[2], corner_low, core[4])]),
+        (cut, [(a, whole) for a in (y_high, core[3], corner_high, core[5])]),
     ]
     normed_near, cache_near = cache_call(place1, lane1, gain, groups, cache_pieces, rings)
     q_pair = query_call(place1, [normed_mine, normed_near], query_pieces, rings)

time: 235 us -> 254 us (1.081)
  waiting for transfers between devices: 116 us -> 126 us
  starting transfers between devices: 49.7 us -> 58.9 us
    ppermute x40 -> x44, starting transfers between devices: 48.2 us -> 57.9 us  [moved(): return lax.ppermute(block, axis, route)]
    ppermute x40 -> x44, waiting for transfers between devices: 108 us -> 117 us  [moved(): return lax.ppermute(block, axis, route)]
  transfers between devices with their start and end apart: 41 -> 45, of which waited for: 14 -> 15; matrix products, arithmetic and copies ran while one was open for 5% -> 5% of each run, Pallas kernels for 20% -> 19%
where the time goes in v2:
time: 254 us; the launch traced here: 253 us
  waiting for transfers between devices  126 us (50%)
  starting transfers between devices  58.9 us (23%)
  Pallas kernels  49.8 us (20%)
  local copies, waits for them, and re-layouts  14.1 us (6%)
  other arithmetic  3.47 us (1%)
    ppermute x44, waiting for transfers between devices, moved(): return lax.ppermute(block, axis, route)  117 us
    ppermute x44, starting transfers between devices, moved(): return lax.ppermute(block, axis, route)  57.9 us
    pallas_call x4, Pallas kernels, attend(): pl.pallas_call(functools.partial(attend_kernel, arrays=arrays, groups=tup...  28.8 us
    ppermute x1, waiting for transfers between devices, paired_layer(): corner = lax.ppermute(o_theirs, ('seq', 'head'), route)  8.92 us
    pallas_call x2, Pallas kernels, cache_call(): pl.pallas_call(kernel, out_shape=[jax.ShapeDtypeStruct((total, wide), jnp...  8.86 us
    pallas_call x2, Pallas kernels, project_call(): pl.pallas_call(kernel, grid_spec=pltpu.PrefetchScalarGridSpec(num_scalar_...  7.74 us
    dynamic_slice x2, local copies, waits for them, and re-layouts, paired_layer(): piece = lax.dynamic_slice_in_dim(source, (lane ^ step) * own, own, 1)  5.6 us
    dynamic_slice x4, local copies, waits for them, and re-layouts, paired_layer(): column = lambda a, at, size: lax.dynamic_slice_in_dim(a, at, size, 1)  5.28 us
  transfers between devices with their start and end apart: 45, of which 15 were waited for; matrix products, arithmetic and copies ran while one was open for 5% of the time, Pallas kernels for 19%

profile of v2, /device:TPU:0, one launch (start us, length us, event | category | flops | bytes accessed | tf_op | source)
XLA Modules:
  0.0 253.0 jit_solution(5357510384741648139)
XLA Ops:
  5.4 3.5 %collective-permute-start.1 = (bf16[512,768]{1,0:T(8,128)(2,1)S(1)}, bf16[512,768]{1,0:T(8,128)(2,1)S(1)}, u32[]{:S(2)}, u32[]{:S(2)}) collective-permute-start(bf16[512,768]{1,0:T(8,128)(2,1)S(1)} %pad_maximum_fusion.refs_2_), channel_id=1, source_target_pairs={{0,8},{4,12},{8,16},{12,20},{16,24},{20,28},{1,9},{5,13},{9,17},{1... | collective-permute-start | bytes 2359304 | tf_op jit(solution)/shard_map/ppermute | solution.py:25
  8.9 13.9 %collective-permute-done.2.refs_3_ = bf16[512,768]{1,0:T(8,128)(2,1)S(1)} collective-permute-done((bf16[512,768]{1,0:T(8,128)(2,1)S(1)}, bf16[512,768]{1,0:T(8,128)(2,1)S(1)}, u32[]{:S(2)}, u32[]{:S(2)}) %collective-permute-start.2) | collective-permute-done | bytes 786464 | tf_op jit(solution)/shard_map/ppermute | solution.py:25
  22.8 3.7 %collective-permute-start.3 = (bf16[512,768]{1,0:T(8,128)(2,1)S(1)}, bf16[512,768]{1,0:T(8,128)(2,1)S(1)}, u32[]{:S(2)}, u32[]{:S(2)}) collective-permute-start(bf16[512,768]{1,0:T(8,128)(2,1)S(1)} %collective-permute-done.2.refs_3_), channel_id=1, source_target_pairs={{0,8},{4,12},{8,16},{12,20},{16,24},{20,28},{1,9},{5,13},{9,17},{1... | collective-permute-start | bytes 2359304 | tf_op jit(solution)/shard_map/ppermute | solution.py:25
  47.5 4.3 %collective-permute-done.20 = bf16[384,640]{1,0:T(8,128)(2,1)} collective-permute-done((bf16[384,640]{1,0:T(8,128)(2,1)}, bf16[384,640]{1,0:T(8,128)(2,1)}, u32[]{:S(2)}, u32[]{:S(2)}) %collective-permute-start.20) | collective-permute-done | bytes 491552 | tf_op jit(solution)/shard_map/ppermute | solution.py:25
  53.0 6.5 %collective-permute-done.refs_1_ = bf16[512,384]{1,0:T(8,128)(2,1)} collective-permute-done((bf16[512,384]{1,0:T(8,128)(2,1)}, bf16[512,384]{1,0:T(8,128)(2,1)}, u32[]{:S(2)}, u32[]{:S(2)}) %collective-permute-start) | collective-permute-done | bytes 393248 | tf_op jit(solution)/shard_map/ppermute | solution.py:25
  63.0 11.6 %attend.4 = (bf16[512,384]{1,0:T(8,128)(2,1)S(1)}, bf16[512,384]{1,0:T(8,128)(2,1)S(1)}, f32[512,128]{1,0:T(8,128)S(1)}, f32[512,384]{1,0:T(8,128)S(1)}) custom-call(s32[1]{0:T(128)} %bitcast.place_ref, s32[8]{0:T(128)S(1)} %copy-done.5, s32[8]{0:T(128)S(1)} %copy-done.6, bf16[512,384]{1,0:T(8,128)(2,1)S(1)} %get-tuple-element.51.refs_0_, ...), custom_call_target="tpu_custom_call" | custom-call | tf_op jit(solution)/shard_map/attend/pallas_call | solution.py:191
  74.6 3.7 %attend.5 = (bf16[512,384]{1,0:T(8,128)(2,1)S(1)}, bf16[512,384]{1,0:T(8,128)(2,1)S(1)}) custom-call(s32[1]{0:T(128)} %bitcast.place_ref, s32[8]{0:T(128)S(1)} %copy-done.5, s32[8]{0:T(128)S(1)} %copy-done.6, bf16[512,384]{1,0:T(8,128)(2,1)S(1)} %get-tuple-element.51.refs_0_, bf16[512,384]{1,0:T(8,128)(2,1)} %collective-permute-done.refs_1_, ...), custom_call_target="tpu_custom_call" | custom-call | tf_op jit(solution)/shard_map/attend/pallas_call | solution.py:191
  81.9 4.8 %collective-permute-done.5.refs_1_ = bf16[512,384]{1,0:T(8,128)(2,1)S(1)} collective-permute-done((bf16[512,384]{1,0:T(8,128)(2,1)S(1)}, bf16[512,384]{1,0:T(8,128)(2,1)S(1)}, u32[]{:S(2)}, u32[]{:S(2)}) %collective-permute-start.5) | collective-permute-done | bytes 393248 | tf_op jit(solution)/shard_map/ppermute | solution.py:25
  86.6 8.3 %collective-permute-done.9.refs_0_ = bf16[512,384]{1,0:T(8,128)(2,1)S(1)} collective-permute-done((bf16[512,384]{1,0:T(8,128)(2,1)S(1)}, bf16[512,384]{1,0:T(8,128)(2,1)S(1)}, u32[]{:S(2)}, u32[]{:S(2)}) %collective-permute-start.9) | collective-permute-done | bytes 393248 | tf_op jit(solution)/shard_map/ppermute | solution.py:25
  95.0 8.9 %collective-permute-done.10.refs_1_ = bf16[512,384]{1,0:T(8,128)(2,1)S(1)} collective-permute-done((bf16[512,384]{1,0:T(8,128)(2,1)S(1)}, bf16[512,384]{1,0:T(8,128)(2,1)S(1)}, u32[]{:S(2)}, u32[]{:S(2)}) %collective-permute-start.10) | collective-permute-done | bytes 393248 | tf_op jit(solution)/shard_map/ppermute | solution.py:498
  107.1 7.4 %collective-permute-start.35 = (bf16[768,384]{1,0:T(8,128)(2,1)S(1)}, bf16[768,384]{1,0:T(8,128)(2,1)S(1)}, u32[]{:S(2)}, u32[]{:S(2)}) collective-permute-start(bf16[768,384]{1,0:T(8,128)(2,1)S(1)} %maximum_select_fusion.1.refs_2_), channel_id=1, source_target_pairs={{0,8},{4,12},{8,16},{12,20},{16,24},{20,28},{1,9},{5,13},{9,17},{1... | collective-permute-start | bytes 1769480 | tf_op jit(solution)/shard_map/ppermute | solution.py:25
  120.6 4.5 %project.3 = (bf16[512,768]{1,0:T(8,128)(2,1)}, bf16[256,768]{1,0:T(8,128)(2,1)S(1)}, bf16[256,768]{1,0:T(8,128)(2,1)S(1)}) custom-call(s32[2]{0:T(128)S(1)} %pad_add_fusion.places_ref, f32[512,768]{1,0:T(8,128)S(1)} %project.2.base_ref, bf16[512,384]{1,0:T(8,128)(2,1)S(1)} %collective-permute-done.9.refs_0_, ...), custom_call_target="tpu_custom_call" | custom-call | tf_op jit(solution)/shard_map/project/pallas_call | solution.py:238
  127.3 17.5 %collective-permute-done.24.refs_12_ = bf16[768,256]{1,0:T(8,128)(2,1)S(1)} collective-permute-done((bf16[768,256]{1,0:T(8,128)(2,1)S(1)}, bf16[768,256]{1,0:T(8,128)(2,1)S(1)}, u32[]{:S(2)}, u32[]{:S(2)}) %collective-permute-start.24) | collective-permute-done | bytes 393248 | tf_op jit(solution)/shard_map/ppermute | solution.py:25
  148.9 7.9 %collective-permute-done.31.refs_4_ = bf16[256,768]{1,0:T(8,128)(2,1)S(1)} collective-permute-done((bf16[256,768]{1,0:T(8,128)(2,1)S(1)}, bf16[256,768]{1,0:T(8,128)(2,1)S(1)}, u32[]{:S(2)}, u32[]{:S(2)}) %collective-permute-start.31) | collective-permute-done | bytes 393248 | tf_op jit(solution)/shard_map/ppermute | solution.py:25
  158.3 6.9 %collective-permute-done.27.refs_0_ = bf16[256,768]{1,0:T(8,128)(2,1)S(1)} collective-permute-done((bf16[256,768]{1,0:T(8,128)(2,1)S(1)}, bf16[256,768]{1,0:T(8,128)(2,1)S(1)}, u32[]{:S(2)}, u32[]{:S(2)}) %collective-permute-start.27) | collective-permute-done | bytes 393248 | tf_op jit(solution)/shard_map/ppermute | solution.py:25
  165.7 6.0 %collective-permute-done.29.refs_2_ = bf16[256,768]{1,0:T(8,128)(2,1)S(1)} collective-permute-done((bf16[256,768]{1,0:T(8,128)(2,1)S(1)}, bf16[256,768]{1,0:T(8,128)(2,1)S(1)}, u32[]{:S(2)}, u32[]{:S(2)}) %collective-permute-start.29) | collective-permute-done | bytes 393248 | tf_op jit(solution)/shard_map/ppermute | solution.py:25
  176.0 4.4 %cache.2 = (bf16[512,3072]{1,0:T(8,128)(2,1)S(1)}, bf16[512,256]{1,0:T(8,128)(2,1)S(1)}) custom-call(s32[1]{0:T(128)} %bitcast.place_ref, s32[1]{0:T(128)} %bitcast.1.lane_ref, f32[1,3072]{1,0:T(1,128)S(1)} %bitcast.5, bf16[512,768]{1,0:T(8,128)(2,1)S(1)} %copy-done, bf16[512,768]{1,0:T(8,128)(2,1)S(1)} %collective-permute-done.15.refs_1_.refs_5_, ...), custom_call_target="tpu_custom_call" | custom-call | tf_op jit(solution)/shard_map/cache/pallas_call | solution.py:327
  180.4 4.9 %collective-permute-start.41 = (bf16[512,256]{1,0:T(8,128)(2,1)S(1)}, bf16[512,256]{1,0:T(8,128)(2,1)S(1)}, u32[]{:S(2)}, u32[]{:S(2)}) collective-permute-start(bf16[512,256]{1,0:T(8,128)(2,1)S(1)} %get-tuple-element.36.refs_2_), channel_id=1, source_target_pairs={{0,8},{4,12},{8,16},{12,20},{16,24},{20,28},{1,9},{5,13},{9,17},{1... | collective-permute-start | bytes 786440 | tf_op jit(solution)/shard_map/ppermute | solution.py:25
  185.4 4.4 %cache.3 = (bf16[512,3072]{1,0:T(8,128)(2,1)S(1)}, bf16[512,256]{1,0:T(8,128)(2,1)S(1)}) custom-call(s32[1]{0:T(128)} %bitcast.place_ref, s32[1]{0:T(128)} %bitcast.1.lane_ref, f32[1,3072]{1,0:T(1,128)S(1)} %bitcast.6, bf16[256,768]{1,0:T(8,128)(2,1)S(1)} %collective-permute-done.27.refs_0_, bf16[256,768]{1,0:T(8,128)(2,1)S(1)} %collective-permute-done.28.refs_1_, ...), custom_call_target="tpu_custom_call" | custom-call | tf_op jit(solution)/shard_map/cache/pallas_call | solution.py:327
  198.9 12.3 %collective-permute-done.40.refs_8_ = bf16[768,384]{1,0:T(8,128)(2,1)S(1)} collective-permute-done((bf16[768,384]{1,0:T(8,128)(2,1)S(1)}, bf16[768,384]{1,0:T(8,128)(2,1)S(1)}, u32[]{:S(2)}, u32[]{:S(2)}) %collective-permute-start.40) | collective-permute-done | bytes 589856 | tf_op jit(solution)/shard_map/ppermute | solution.py:25
  211.2 12.0 %collective-permute-done.38.refs_6_ = bf16[768,384]{1,0:T(8,128)(2,1)S(1)} collective-permute-done((bf16[768,384]{1,0:T(8,128)(2,1)S(1)}, bf16[768,384]{1,0:T(8,128)(2,1)S(1)}, u32[]{:S(2)}, u32[]{:S(2)}) %collective-permute-start.38) | collective-permute-done | bytes 589856 | tf_op jit(solution)/shard_map/ppermute | solution.py:25
  223.2 4.4 %queries.1 = (bf16[512,384]{1,0:T(8,128)(2,1)S(1)}, bf16[512,384]{1,0:T(8,128)(2,1)S(1)}) custom-call(s32[1]{0:T(128)} %bitcast.place_ref, bf16[512,3072]{1,0:T(8,128)(2,1)S(1)} %get-tuple-element.32.refs_0_, bf16[512,3072]{1,0:T(8,128)(2,1)S(1)} %get-tuple-element.33.refs_1_, bf16[768,384]{1,0:T(8,128)(2,1)S(1)} %maximum_select_fusion.1.refs_2_, ...), custom_call_target="tpu_custom_call" | custom-call | tf_op jit(solution)/shard_map/queries/pallas_call | solution.py:363
  227.7 10.7 %attend.6 = (bf16[512,384]{1,0:T(8,128)(2,1)S(1)}, bf16[512,384]{1,0:T(8,128)(2,1)S(1)}, f32[512,128]{1,0:T(8,128)S(1)}, f32[512,384]{1,0:T(8,128)S(1)}) custom-call(s32[1]{0:T(128)} %bitcast.place_ref, s32[8]{0:T(128)S(1)} %copy-done.5, s32[8]{0:T(128)S(1)} %copy-done.6, bf16[512,384]{1,0:T(8,128)(2,1)S(1)} %get-tuple-element.34.refs_0_, ...), custom_call_target="tpu_custom_call" | custom-call | tf_op jit(solution)/shard_map/attend/pallas_call | solution.py:191
  241.9 10.0 %collective-permute-done.44 = bf16[512,384]{1,0:T(8,128)(2,1)S(1)} collective-permute-done((bf16[512,384]{1,0:T(8,128)(2,1)S(1)}, bf16[512,384]{1,0:T(8,128)(2,1)S(1)}, u32[]{:S(2)}, u32[]{:S(2)}) %collective-permute-start.44) | collective-permute-done | bytes 393248 | tf_op jit(solution)/shard_map/ppermute | solution.py:25
  (115 shorter events, 69.1 us)
Async XLA Ops:
  2.2 20.6 %collective-permute-start.2 = (bf16[512,768]{1,0:T(8,128)(2,1)S(1)}, bf16[512,768]{1,0:T(8,128)(2,1)S(1)}, u32[]{:S(2)}, u32[]{:S(2)}) collective-permute-start(bf16[512,768]{1,0:T(8,128)(2,1)S(1)} %pad_maximum_fusion.1), channel_id=1, source_target_pairs={{0,4},{4,0},{8,12},{12,8},{16,20},{20,16},{24,28},{28,24},{1,5},{5... | collective-permute-start | bytes 2359304 | tf_op jit(solution)/shard_map/ppermute | solution.py:25
  5.4 33.6 %collective-permute-start.1 = (bf16[512,768]{1,0:T(8,128)(2,1)S(1)}, bf16[512,768]{1,0:T(8,128)(2,1)S(1)}, u32[]{:S(2)}, u32[]{:S(2)}) collective-permute-start(bf16[512,768]{1,0:T(8,128)(2,1)S(1)} %pad_maximum_fusion.refs_2_), channel_id=1, source_target_pairs={{0,8},{4,12},{8,16},{12,20},{16,24},{20,28},{1,9},{5,13},{9,17},{1... | collective-permute-start | bytes 2359304 | tf_op jit(solution)/shard_map/ppermute | solution.py:25
  29.0 52.0 %collective-permute-start.8 = (bf16[768,768]{1,0:T(8,128)(2,1)}, bf16[768,768]{1,0:T(8,128)(2,1)}, u32[]{:S(2)}, u32[]{:S(2)}) collective-permute-start(bf16[768,768]{1,0:T(8,128)(2,1)} %constant_dynamic-slice_fusion.8), channel_id=1, source_target_pairs={{0,1},{1,0},{2,3},{3,2},{4,5},{5,4},{6,7},{7,6},{8,9},{9,8},{10,11... | collective-permute-start | bytes 3538952 | tf_op jit(solution)/shard_map/ppermute | solution.py:25
  32.2 49.7 %collective-permute-start.13 = (bf16[768,768]{1,0:T(8,128)(2,1)}, bf16[768,768]{1,0:T(8,128)(2,1)}, u32[]{:S(2)}, u32[]{:S(2)}) collective-permute-start(bf16[768,768]{1,0:T(8,128)(2,1)} %get-tuple-element.45), channel_id=1, source_target_pairs={{0,2},{1,3},{2,0},{3,1},{4,6},{5,7},{6,4},{7,5},{8,10},{9,11},{10,... | collective-permute-start | bytes 3538952 | tf_op jit(solution)/shard_map/ppermute | solution.py:25
  43.4 31.2 %collective-permute-start.4 = (bf16[512,768]{1,0:T(8,128)(2,1)}, bf16[512,768]{1,0:T(8,128)(2,1)}, u32[]{:S(2)}, u32[]{:S(2)}) collective-permute-start(bf16[512,768]{1,0:T(8,128)(2,1)} %broadcast_select_fusion), channel_id=1, source_target_pairs={{8,16},{12,20},{16,24},{20,28},{9,17},{13,21},{17,25},{21,29},{10,... | collective-permute-start | bytes 2359304 | tf_op jit(solution)/shard_map/ppermute | solution.py:25
  51.8 52.0 %collective-permute-start.14 = (bf16[768,768]{1,0:T(8,128)(2,1)}, bf16[768,768]{1,0:T(8,128)(2,1)}, u32[]{:S(2)}, u32[]{:S(2)}) collective-permute-start(bf16[768,768]{1,0:T(8,128)(2,1)} %get-tuple-element.44), channel_id=1, source_target_pairs={{0,3},{1,2},{2,1},{3,0},{4,7},{5,6},{6,5},{7,4},{8,11},{9,10},{10,... | collective-permute-start | bytes 3538952 | tf_op jit(solution)/shard_map/ppermute | solution.py:25
  59.5 20.4 %collective-permute-start.21 = (bf16[768,256]{1,0:T(8,128)(2,1)S(1)}, bf16[768,256]{1,0:T(8,128)(2,1)S(1)}, u32[]{:S(2)}, u32[]{:S(2)}) collective-permute-start(bf16[768,256]{1,0:T(8,128)(2,1)S(1)} %maximum_select_fusion.2.refs_8_), channel_id=1, source_target_pairs={{0,8},{4,12},{8,16},{12,20},{16,24},{20,28},{1,9},{5,13},{9,17},{1... | collective-permute-start | bytes 1179656 | tf_op jit(solution)/shard_map/ppermute | solution.py:25
  80.9 23.0 %collective-permute-start.10 = (bf16[512,384]{1,0:T(8,128)(2,1)S(1)}, bf16[512,384]{1,0:T(8,128)(2,1)S(1)}, u32[]{:S(2)}, u32[]{:S(2)}) collective-permute-start(bf16[512,384]{1,0:T(8,128)(2,1)S(1)} %get-tuple-element.28), channel_id=1, source_target_pairs={{0,6},{1,7},{2,4},{3,5},{4,2},{5,3},{6,0},{7,1},{8,14},{9,15},{10,... | collective-permute-start | bytes 1179656 | tf_op jit(solution)/shard_map/ppermute | solution.py:498
  81.9 23.3 %collective-permute-start.6 = (bf16[512,384]{1,0:T(8,128)(2,1)S(1)}, bf16[512,384]{1,0:T(8,128)(2,1)S(1)}, u32[]{:S(2)}, u32[]{:S(2)}) collective-permute-start(bf16[512,384]{1,0:T(8,128)(2,1)S(1)} %get-tuple-element.27.refs_0_), channel_id=1, source_target_pairs={{0,1},{1,0},{2,3},{3,2},{4,5},{5,4},{6,7},{7,6},{8,9},{9,8},{10,11... | collective-permute-start | bytes 1179656 | tf_op jit(solution)/shard_map/ppermute | solution.py:25
  86.6 20.5 %collective-permute-start.7 = (bf16[512,384]{1,0:T(8,128)(2,1)S(1)}, bf16[512,384]{1,0:T(8,128)(2,1)S(1)}, u32[]{:S(2)}, u32[]{:S(2)}) collective-permute-start(bf16[512,384]{1,0:T(8,128)(2,1)S(1)} %collective-permute-done.5.refs_1_), channel_id=1, source_target_pairs={{0,1},{1,0},{2,3},{3,2},{4,5},{5,4},{6,7},{7,6},{8,9},{9,8},{10,11... | collective-permute-start | bytes 1179656 | tf_op jit(solution)/shard_map/ppermute | solution.py:25
  103.9 21.2 %collective-permute-start.22 = (bf16[768,256]{1,0:T(8,128)(2,1)S(1)}, bf16[768,256]{1,0:T(8,128)(2,1)S(1)}, u32[]{:S(2)}, u32[]{:S(2)}) collective-permute-start(bf16[768,256]{1,0:T(8,128)(2,1)S(1)} %maximum_select_fusion.2.refs_8_), channel_id=1, source_target_pairs={{8,0},{12,4},{16,8},{20,12},{24,16},{28,20},{9,1},{13,5},{17,9},{2... | collective-permute-start | bytes 1179656 | tf_op jit(solution)/shard_map/ppermute | solution.py:25
  105.2 21.4 %collective-permute-start.23 = (bf16[768,256]{1,0:T(8,128)(2,1)S(1)}, bf16[768,256]{1,0:T(8,128)(2,1)S(1)}, u32[]{:S(2)}, u32[]{:S(2)}) collective-permute-start(bf16[768,256]{1,0:T(8,128)(2,1)S(1)} %collective-permute-done.21.refs_9_), channel_id=1, source_target_pairs={{8,16},{12,20},{16,24},{20,28},{9,17},{13,21},{17,25},{21,29},{10,... | collective-permute-start | bytes 1179656 | tf_op jit(solution)/shard_map/ppermute | solution.py:25
  107.1 39.7 %collective-permute-start.35 = (bf16[768,384]{1,0:T(8,128)(2,1)S(1)}, bf16[768,384]{1,0:T(8,128)(2,1)S(1)}, u32[]{:S(2)}, u32[]{:S(2)}) collective-permute-start(bf16[768,384]{1,0:T(8,128)(2,1)S(1)} %maximum_select_fusion.1.refs_2_), channel_id=1, source_target_pairs={{0,8},{4,12},{8,16},{12,20},{16,24},{20,28},{1,9},{5,13},{9,17},{1... | collective-permute-start | bytes 1769480 | tf_op jit(solution)/shard_map/ppermute | solution.py:25
  114.5 30.3 %collective-permute-start.24 = (bf16[768,256]{1,0:T(8,128)(2,1)S(1)}, bf16[768,256]{1,0:T(8,128)(2,1)S(1)}, u32[]{:S(2)}, u32[]{:S(2)}) collective-permute-start(bf16[768,256]{1,0:T(8,128)(2,1)S(1)} %maximum_select_fusion.2.refs_8_), channel_id=1, source_target_pairs={{16,0},{20,4},{24,8},{28,12},{17,1},{21,5},{25,9},{29,13},{18,2},{... | collective-permute-start | bytes 1179656 | tf_op jit(solution)/shard_map/ppermute | solution.py:25
  115.8 29.5 %collective-permute-start.26 = (bf16[768,256]{1,0:T(8,128)(2,1)S(1)}, bf16[768,256]{1,0:T(8,128)(2,1)S(1)}, u32[]{:S(2)}, u32[]{:S(2)}) collective-permute-start(bf16[768,256]{1,0:T(8,128)(2,1)S(1)} %maximum_select_fusion.2.refs_8_), channel_id=1, source_target_pairs={{24,0},{28,4},{25,1},{29,5},{26,2},{30,6},{27,3},{31,7}} | collective-permute-start | bytes 1179656 | tf_op jit(solution)/shard_map/ppermute | solution.py:25
  125.1 23.2 %collective-permute-start.16 = (bf16[256,768]{1,0:T(8,128)(2,1)S(1)}, bf16[256,768]{1,0:T(8,128)(2,1)S(1)}, u32[]{:S(2)}, u32[]{:S(2)}) collective-permute-start(bf16[256,768]{1,0:T(8,128)(2,1)S(1)} %get-tuple-element.30), channel_id=1, source_target_pairs={{0,2},{1,3},{2,0},{3,1},{4,6},{5,7},{6,4},{7,5},{8,10},{9,11},{10,... | collective-permute-start | bytes 1179656 | tf_op jit(solution)/shard_map/ppermute | solution.py:25
  126.6 22.2 %collective-permute-start.25 = (bf16[768,256]{1,0:T(8,128)(2,1)S(1)}, bf16[768,256]{1,0:T(8,128)(2,1)S(1)}, u32[]{:S(2)}, u32[]{:S(2)}) collective-permute-start(bf16[768,256]{1,0:T(8,128)(2,1)S(1)} %collective-permute-done.23.refs_11_), channel_id=1, source_target_pairs={{16,24},{20,28},{17,25},{21,29},{18,26},{22,30},{19,27},{23,31}} | collective-permute-start | bytes 1179656 | tf_op jit(solution)/shard_map/ppermute | solution.py:25
  148.3 23.4 %collective-permute-start.29 = (bf16[256,768]{1,0:T(8,128)(2,1)S(1)}, bf16[256,768]{1,0:T(8,128)(2,1)S(1)}, u32[]{:S(2)}, u32[]{:S(2)}) collective-permute-start(bf16[256,768]{1,0:T(8,128)(2,1)S(1)} %collective-permute-done.16.refs_2_), channel_id=1, source_target_pairs={{0,4},{4,0},{8,12},{12,8},{16,20},{20,16},{24,28},{28,24},{1,5},{5... | collective-permute-start | bytes 1179656 | tf_op jit(solution)/shard_map/ppermute | solution.py:25
  148.9 25.6 %collective-permute-start.15 = (bf16[512,768]{1,0:T(8,128)(2,1)}, bf16[512,768]{1,0:T(8,128)(2,1)S(1)}, u32[]{:S(2)}, u32[]{:S(2)}) collective-permute-start(bf16[512,768]{1,0:T(8,128)(2,1)} %get-tuple-element.21.refs_0_.refs_4_), channel_id=1, source_target_pairs={{0,1},{1,0},{2,3},{3,2},{4,5},{5,4},{6,7},{7,6},{8,9},{9,8},{10,11... | collective-permute-start | bytes 2359304 | tf_op jit(solution)/shard_map/ppermute | solution.py:25
  171.7 21.9 %collective-permute-start.36 = (bf16[768,384]{1,0:T(8,128)(2,1)S(1)}, bf16[768,384]{1,0:T(8,128)(2,1)S(1)}, u32[]{:S(2)}, u32[]{:S(2)}) collective-permute-start(bf16[768,384]{1,0:T(8,128)(2,1)S(1)} %maximum_select_fusion.1.refs_2_), channel_id=1, source_target_pairs={{8,0},{12,4},{16,8},{20,12},{24,16},{28,20},{9,1},{13,5},{17,9},{2... | collective-permute-start | bytes 1769480 | tf_op jit(solution)/shard_map/ppermute | solution.py:25
  173.0 21.9 %collective-permute-start.37 = (bf16[768,384]{1,0:T(8,128)(2,1)S(1)}, bf16[768,384]{1,0:T(8,128)(2,1)S(1)}, u32[]{:S(2)}, u32[]{:S(2)}) collective-permute-start(bf16[768,384]{1,0:T(8,128)(2,1)S(1)} %collective-permute-done.35.refs_3_), channel_id=1, source_target_pairs={{8,16},{12,20},{16,24},{20,28},{9,17},{13,21},{17,25},{21,29},{10,... | collective-permute-start | bytes 1769480 | tf_op jit(solution)/shard_map/ppermute | solution.py:25
  193.6 29.6 %collective-permute-start.38 = (bf16[768,384]{1,0:T(8,128)(2,1)S(1)}, bf16[768,384]{1,0:T(8,128)(2,1)S(1)}, u32[]{:S(2)}, u32[]{:S(2)}) collective-permute-start(bf16[768,384]{1,0:T(8,128)(2,1)S(1)} %collective-permute-done.36.refs_4_), channel_id=1, source_target_pairs={{8,0},{12,4},{16,8},{20,12},{9,1},{13,5},{17,9},{21,13},{10,2},{14... | collective-permute-start | bytes 1769480 | tf_op jit(solution)/shard_map/ppermute | solution.py:25
  194.9 28.3 %collective-permute-start.39 = (bf16[768,384]{1,0:T(8,128)(2,1)S(1)}, bf16[768,384]{1,0:T(8,128)(2,1)S(1)}, u32[]{:S(2)}, u32[]{:S(2)}) collective-permute-start(bf16[768,384]{1,0:T(8,128)(2,1)S(1)} %collective-permute-done.37.refs_5_), channel_id=1, source_target_pairs={{16,24},{20,28},{17,25},{21,29},{18,26},{22,30},{19,27},{23,31}} | collective-permute-start | bytes 1769480 | tf_op jit(solution)/shard_map/ppermute | solution.py:25
  198.2 40.2 %collective-permute-start.43 = (bf16[512,256]{1,0:T(8,128)(2,1)S(1)}, bf16[512,256]{1,0:T(8,128)(2,1)S(1)}, u32[]{:S(2)}, u32[]{:S(2)}) collective-permute-start(bf16[512,256]{1,0:T(8,128)(2,1)S(1)} %broadcast_select_fusion.1), channel_id=1, source_target_pairs={{8,16},{12,20},{16,24},{20,28},{9,17},{13,21},{17,25},{21,29},{10,... | collective-permute-start | bytes 786440 | tf_op jit(solution)/shard_map/ppermute | solution.py:25
  (32 other events, 587.2 us)

commit v3 on v2

--- a/solution.py
+++ b/solution.py
@@ -376,6 +376,34 @@
     )(place1, *normed, *[pieces[n] for n in names])
 
 
+def beside_call(which, a, b):
+    rows, wide = a.shape
+    half = wide // 2
+
+    def kernel(which_ref, a_ref, b_ref, o_ref, sems):
+        part = pl.ds(pl.multiple_of(which_ref[0] * half, HEAD_DIM), half)
+        copies = [
+            pltpu.make_async_copy(
+                ref.at[:, part], o_ref.at[:, n * half : (n + 1) * half], sems.at[n]
+            )
+            for n, ref in enumerate((a_ref, b_ref))
+        ]
+        for copy in copies:
+            copy.start()
+        for copy in copies:
+            copy.wait()
+
+    anywhere = pl.BlockSpec(memory_space=pl.ANY)
+    return pl.pallas_call(
+        kernel,
+        out_shape=jax.ShapeDtypeStruct((rows, wide), a.dtype),
+        in_specs=[pl.BlockSpec(memory_space=pltpu.SMEM), anywhere, anywhere],
+        out_specs=anywhere,
+        scratch_shapes=[pltpu.SemaphoreType.DMA((2,))],
+        name="beside",
+    )(which, a, b)
+
+
 def paired_layer(
     residual,
     q_self,
@@ -412,8 +440,7 @@
     column = lambda a, at, size: lax.dynamic_slice_in_dim(a, at, size, 1)
 
     def kv_of(which):
-        at = which * half
-        return jnp.concatenate([column(k_self, at, half), column(v_self, at, half)], axis=1)
+        return beside_call(which[None], k_self, v_self)
 
     mine, theirs = kv_of(side), kv_of(1 - side)
     q_mine = column(q_self, side * half, half)

time: 254 us -> 296 us (1.17)
  Pallas kernels: 49.8 us -> 99.8 us
  waiting for transfers between devices: 126 us -> 122 us
    pallas_call x0 -> x2, Pallas kernels: none -> 49.9 us  [beside_call(): pl.pallas_call(kernel, out_shape=jax.ShapeDtypeStruct((rows, wide), a.dty...]
    ppermute x1, waiting for transfers between devices: 8.92 us -> 5.54 us  [paired_layer(): corner = lax.ppermute(o_theirs, ('seq', 'head'), route)]
  transfers between devices with their start and end apart: 45 -> 45, of which waited for: 15 -> 14; matrix products, arithmetic and copies ran while one was open for 5% -> 4% of each run, Pallas kernels for 19% -> 24%
where the time goes in v3:
time: 296 us; the launch traced here: 295 us
  waiting for transfers between devices  122 us (41%)
  Pallas kernels  99.8 us (34%)
  starting transfers between devices  57.5 us (19%)
  local copies, waits for them, and re-layouts  11.5 us (4%)
  other arithmetic  3.34 us (1%)
    ppermute x44, waiting for transfers between devices, moved(): return lax.ppermute(block, axis, route)  116 us
    ppermute x44, starting transfers between devices, moved(): return lax.ppermute(block, axis, route)  55.9 us
    pallas_call x2, Pallas kernels, beside_call(): pl.pallas_call(kernel, out_shape=jax.ShapeDtypeStruct((rows, wide), a.dty...  49.9 us
    pallas_call x4, Pallas kernels, attend(): pl.pallas_call(functools.partial(attend_kernel, arrays=arrays, groups=tup...  28.8 us
    pallas_call x2, Pallas kernels, cache_call(): pl.pallas_call(kernel, out_shape=[jax.ShapeDtypeStruct((total, wide), jnp...  8.91 us
    pallas_call x2, Pallas kernels, project_call(): pl.pallas_call(kernel, grid_spec=pltpu.PrefetchScalarGridSpec(num_scalar_...  7.78 us
  transfers between devices with their start and end apart: 45, of which 14 were waited for; matrix products, arithmetic and copies ran while one was open for 4% of the time, Pallas kernels for 24%

profile of v3, /device:TPU:0, one launch (start us, length us, event | category | flops | bytes accessed | tf_op | source)
XLA Modules:
  0.0 294.8 jit_solution(3995045444219086555)
XLA Ops:
  0.6 24.9 %beside.3 = bf16[512,768]{1,0:T(8,128)(2,1)} custom-call(s32[1]{0:T(128)} %bitcast.3.which_ref, bf16[512,768]{1,0:T(8,128)(2,1)} %a_ref.3, bf16[512,768]{1,0:T(8,128)(2,1)} %b_ref.3), custom_call_target="tpu_custom_call" | custom-call | tf_op jit(solution)/shard_map/beside/pallas_call | solution.py:397
  28.7 24.9 %beside.2.refs_2_ = bf16[512,768]{1,0:T(8,128)(2,1)} custom-call(s32[1]{0:T(128)} %bitcast.2.which_ref, bf16[512,768]{1,0:T(8,128)(2,1)} %a_ref.3, bf16[512,768]{1,0:T(8,128)(2,1)} %b_ref.3), custom_call_target="tpu_custom_call" | custom-call | tf_op jit(solution)/shard_map/beside/pallas_call | solution.py:397
  71.0 4.3 %collective-permute-done.1.refs_4_ = bf16[512,768]{1,0:T(8,128)(2,1)S(1)} collective-permute-done((bf16[512,768]{1,0:T(8,128)(2,1)}, bf16[512,768]{1,0:T(8,128)(2,1)S(1)}, u32[]{:S(2)}, u32[]{:S(2)}) %collective-permute-start.1) | collective-permute-done | bytes 786464 | tf_op jit(solution)/shard_map/ppermute | solution.py:25
  75.3 15.3 %collective-permute-done.3.refs_5_ = bf16[512,768]{1,0:T(8,128)(2,1)S(1)} collective-permute-done((bf16[512,768]{1,0:T(8,128)(2,1)S(1)}, bf16[512,768]{1,0:T(8,128)(2,1)S(1)}, u32[]{:S(2)}, u32[]{:S(2)}) %collective-permute-start.3) | collective-permute-done | bytes 786464 | tf_op jit(solution)/shard_map/ppermute | solution.py:25
  95.9 8.4 %collective-permute-done.refs_1_ = bf16[512,384]{1,0:T(8,128)(2,1)} collective-permute-done((bf16[512,384]{1,0:T(8,128)(2,1)}, bf16[512,384]{1,0:T(8,128)(2,1)}, u32[]{:S(2)}, u32[]{:S(2)}) %collective-permute-start) | collective-permute-done | bytes 393248 | tf_op jit(solution)/shard_map/ppermute | solution.py:25
  104.3 7.0 %collective-permute-start.21 = (bf16[768,256]{1,0:T(8,128)(2,1)S(1)}, bf16[768,256]{1,0:T(8,128)(2,1)S(1)}, u32[]{:S(2)}, u32[]{:S(2)}) collective-permute-start(bf16[768,256]{1,0:T(8,128)(2,1)S(1)} %maximum_select_fusion.2.refs_8_), channel_id=1, source_target_pairs={{0,8},{4,12},{8,16},{12,20},{16,24},{20,28},{1,9},{5,13},{9,17},{1... | collective-permute-start | bytes 1179656 | tf_op jit(solution)/shard_map/ppermute | solution.py:25
  111.4 11.6 %attend.4 = (bf16[512,384]{1,0:T(8,128)(2,1)S(1)}, bf16[512,384]{1,0:T(8,128)(2,1)S(1)}, f32[512,128]{1,0:T(8,128)S(1)}, f32[512,384]{1,0:T(8,128)S(1)}) custom-call(s32[1]{0:T(128)} %bitcast.place_ref, s32[8]{0:T(128)S(1)} %copy-done.6, s32[8]{0:T(128)S(1)} %copy-done.7, bf16[512,384]{1,0:T(8,128)(2,1)S(1)} %get-tuple-element.47.refs_0_, ...), custom_call_target="tpu_custom_call" | custom-call | tf_op jit(solution)/shard_map/attend/pallas_call | solution.py:191
  122.9 3.7 %attend.5 = (bf16[512,384]{1,0:T(8,128)(2,1)S(1)}, bf16[512,384]{1,0:T(8,128)(2,1)S(1)}) custom-call(s32[1]{0:T(128)} %bitcast.place_ref, s32[8]{0:T(128)S(1)} %copy-done.6, s32[8]{0:T(128)S(1)} %copy-done.7, bf16[512,384]{1,0:T(8,128)(2,1)S(1)} %get-tuple-element.47.refs_0_, bf16[512,384]{1,0:T(8,128)(2,1)} %collective-permute-done.refs_1_, ...), custom_call_target="tpu_custom_call" | custom-call | tf_op jit(solution)/shard_map/attend/pallas_call | solution.py:191
  130.2 7.6 %collective-permute-done.5.refs_1_ = bf16[512,384]{1,0:T(8,128)(2,1)S(1)} collective-permute-done((bf16[512,384]{1,0:T(8,128)(2,1)S(1)}, bf16[512,384]{1,0:T(8,128)(2,1)S(1)}, u32[]{:S(2)}, u32[]{:S(2)}) %collective-permute-start.5) | collective-permute-done | bytes 393248 | tf_op jit(solution)/shard_map/ppermute | solution.py:25
  139.2 5.5 %collective-permute-done.10.refs_1_ = bf16[512,384]{1,0:T(8,128)(2,1)S(1)} collective-permute-done((bf16[512,384]{1,0:T(8,128)(2,1)S(1)}, bf16[512,384]{1,0:T(8,128)(2,1)S(1)}, u32[]{:S(2)}, u32[]{:S(2)}) %collective-permute-start.10) | collective-permute-done | bytes 393248 | tf_op jit(solution)/shard_map/ppermute | solution.py:525
  147.9 7.4 %collective-permute-start.35 = (bf16[768,384]{1,0:T(8,128)(2,1)S(1)}, bf16[768,384]{1,0:T(8,128)(2,1)S(1)}, u32[]{:S(2)}, u32[]{:S(2)}) collective-permute-start(bf16[768,384]{1,0:T(8,128)(2,1)S(1)} %maximum_select_fusion.1.refs_2_), channel_id=1, source_target_pairs={{0,8},{4,12},{8,16},{12,20},{16,24},{20,28},{1,9},{5,13},{9,17},{1... | collective-permute-start | bytes 1769480 | tf_op jit(solution)/shard_map/ppermute | solution.py:25
  161.6 4.5 %project.3 = (bf16[512,768]{1,0:T(8,128)(2,1)}, bf16[256,768]{1,0:T(8,128)(2,1)S(1)}, bf16[256,768]{1,0:T(8,128)(2,1)S(1)}) custom-call(s32[2]{0:T(128)S(1)} %pad_add_fusion.places_ref, f32[512,768]{1,0:T(8,128)S(1)} %project.2.base_ref, bf16[512,384]{1,0:T(8,128)(2,1)S(1)} %collective-permute-done.9.refs_0_, ...), custom_call_target="tpu_custom_call" | custom-call | tf_op jit(solution)/shard_map/project/pallas_call | solution.py:238
  167.3 18.4 %collective-permute-done.24.refs_12_ = bf16[768,256]{1,0:T(8,128)(2,1)S(1)} collective-permute-done((bf16[768,256]{1,0:T(8,128)(2,1)S(1)}, bf16[768,256]{1,0:T(8,128)(2,1)S(1)}, u32[]{:S(2)}, u32[]{:S(2)}) %collective-permute-start.24) | collective-permute-done | bytes 393248 | tf_op jit(solution)/shard_map/ppermute | solution.py:25
  188.8 8.9 %collective-permute-done.31.refs_4_ = bf16[256,768]{1,0:T(8,128)(2,1)S(1)} collective-permute-done((bf16[256,768]{1,0:T(8,128)(2,1)S(1)}, bf16[256,768]{1,0:T(8,128)(2,1)S(1)}, u32[]{:S(2)}, u32[]{:S(2)}) %collective-permute-start.31) | collective-permute-done | bytes 393248 | tf_op jit(solution)/shard_map/ppermute | solution.py:25
  198.3 7.8 %collective-permute-done.27.refs_0_ = bf16[256,768]{1,0:T(8,128)(2,1)S(1)} collective-permute-done((bf16[256,768]{1,0:T(8,128)(2,1)S(1)}, bf16[256,768]{1,0:T(8,128)(2,1)S(1)}, u32[]{:S(2)}, u32[]{:S(2)}) %collective-permute-start.27) | collective-permute-done | bytes 393248 | tf_op jit(solution)/shard_map/ppermute | solution.py:25
  206.6 6.9 %collective-permute-done.29.refs_2_ = bf16[256,768]{1,0:T(8,128)(2,1)S(1)} collective-permute-done((bf16[256,768]{1,0:T(8,128)(2,1)S(1)}, bf16[256,768]{1,0:T(8,128)(2,1)S(1)}, u32[]{:S(2)}, u32[]{:S(2)}) %collective-permute-start.29) | collective-permute-done | bytes 393248 | tf_op jit(solution)/shard_map/ppermute | solution.py:25
  217.8 4.4 %cache.2 = (bf16[512,3072]{1,0:T(8,128)(2,1)S(1)}, bf16[512,256]{1,0:T(8,128)(2,1)S(1)}) custom-call(s32[1]{0:T(128)} %bitcast.place_ref, s32[1]{0:T(128)} %bitcast.1.lane_ref, f32[1,3072]{1,0:T(1,128)S(1)} %bitcast.7, bf16[512,768]{1,0:T(8,128)(2,1)S(1)} %copy-done.1, bf16[512,768]{1,0:T(8,128)(2,1)S(1)} %collective-permute-done.15.refs_1_.refs_5_, ...), custom_call_target="tpu_custom_call" | custom-call | tf_op jit(solution)/shard_map/cache/pallas_call | solution.py:327
  222.2 4.9 %collective-permute-start.41 = (bf16[512,256]{1,0:T(8,128)(2,1)S(1)}, bf16[512,256]{1,0:T(8,128)(2,1)S(1)}, u32[]{:S(2)}, u32[]{:S(2)}) collective-permute-start(bf16[512,256]{1,0:T(8,128)(2,1)S(1)} %get-tuple-element.36.refs_2_), channel_id=1, source_target_pairs={{0,8},{4,12},{8,16},{12,20},{16,24},{20,28},{1,9},{5,13},{9,17},{1... | collective-permute-start | bytes 786440 | tf_op jit(solution)/shard_map/ppermute | solution.py:25
  227.2 4.5 %cache.3 = (bf16[512,3072]{1,0:T(8,128)(2,1)S(1)}, bf16[512,256]{1,0:T(8,128)(2,1)S(1)}) custom-call(s32[1]{0:T(128)} %bitcast.place_ref, s32[1]{0:T(128)} %bitcast.1.lane_ref, f32[1,3072]{1,0:T(1,128)S(1)} %bitcast.8, bf16[256,768]{1,0:T(8,128)(2,1)S(1)} %collective-permute-done.27.refs_0_, bf16[256,768]{1,0:T(8,128)(2,1)S(1)} %collective-permute-done.28.refs_1_, ...), custom_call_target="tpu_custom_call" | custom-call | tf_op jit(solution)/shard_map/cache/pallas_call | solution.py:327
  240.7 12.3 %collective-permute-done.40.refs_8_ = bf16[768,384]{1,0:T(8,128)(2,1)S(1)} collective-permute-done((bf16[768,384]{1,0:T(8,128)(2,1)S(1)}, bf16[768,384]{1,0:T(8,128)(2,1)S(1)}, u32[]{:S(2)}, u32[]{:S(2)}) %collective-permute-start.40) | collective-permute-done | bytes 589856 | tf_op jit(solution)/shard_map/ppermute | solution.py:25
  253.0 12.0 %collective-permute-done.38.refs_6_ = bf16[768,384]{1,0:T(8,128)(2,1)S(1)} collective-permute-done((bf16[768,384]{1,0:T(8,128)(2,1)S(1)}, bf16[768,384]{1,0:T(8,128)(2,1)S(1)}, u32[]{:S(2)}, u32[]{:S(2)}) %collective-permute-start.38) | collective-permute-done | bytes 589856 | tf_op jit(solution)/shard_map/ppermute | solution.py:25
  265.1 4.4 %queries.1 = (bf16[512,384]{1,0:T(8,128)(2,1)S(1)}, bf16[512,384]{1,0:T(8,128)(2,1)S(1)}) custom-call(s32[1]{0:T(128)} %bitcast.place_ref, bf16[512,3072]{1,0:T(8,128)(2,1)S(1)} %get-tuple-element.32.refs_0_, bf16[512,3072]{1,0:T(8,128)(2,1)S(1)} %get-tuple-element.33.refs_1_, bf16[768,384]{1,0:T(8,128)(2,1)S(1)} %maximum_select_fusion.1.refs_2_, ...), custom_call_target="tpu_custom_call" | custom-call | tf_op jit(solution)/shard_map/queries/pallas_call | solution.py:363
  269.5 10.7 %attend.6 = (bf16[512,384]{1,0:T(8,128)(2,1)S(1)}, bf16[512,384]{1,0:T(8,128)(2,1)S(1)}, f32[512,128]{1,0:T(8,128)S(1)}, f32[512,384]{1,0:T(8,128)S(1)}) custom-call(s32[1]{0:T(128)} %bitcast.place_ref, s32[8]{0:T(128)S(1)} %copy-done.6, s32[8]{0:T(128)S(1)} %copy-done.7, bf16[512,384]{1,0:T(8,128)(2,1)S(1)} %get-tuple-element.34.refs_0_, ...), custom_call_target="tpu_custom_call" | custom-call | tf_op jit(solution)/shard_map/attend/pallas_call | solution.py:191
  283.7 10.1 %collective-permute-done.44 = bf16[512,384]{1,0:T(8,128)(2,1)S(1)} collective-permute-done((bf16[512,384]{1,0:T(8,128)(2,1)S(1)}, bf16[512,384]{1,0:T(8,128)(2,1)S(1)}, u32[]{:S(2)}, u32[]{:S(2)}) %collective-permute-start.44) | collective-permute-done | bytes 393248 | tf_op jit(solution)/shard_map/ppermute | solution.py:25
  (118 shorter events, 63.1 us)
Async XLA Ops:
  25.6 31.5 %collective-permute-start.2 = (bf16[512,768]{1,0:T(8,128)(2,1)}, bf16[512,768]{1,0:T(8,128)(2,1)S(1)}, u32[]{:S(2)}, u32[]{:S(2)}) collective-permute-start(bf16[512,768]{1,0:T(8,128)(2,1)} %beside.3), channel_id=1, source_target_pairs={{0,4},{4,0},{8,12},{12,8},{16,20},{20,16},{24,28},{28,24},{1,5},{5... | collective-permute-start | bytes 2359304 | tf_op jit(solution)/shard_map/ppermute | solution.py:25
  53.6 21.7 %collective-permute-start.1 = (bf16[512,768]{1,0:T(8,128)(2,1)}, bf16[512,768]{1,0:T(8,128)(2,1)S(1)}, u32[]{:S(2)}, u32[]{:S(2)}) collective-permute-start(bf16[512,768]{1,0:T(8,128)(2,1)} %beside.2.refs_2_), channel_id=1, source_target_pairs={{0,8},{4,12},{8,16},{12,20},{16,24},{20,28},{1,9},{5,13},{9,17},{1... | collective-permute-start | bytes 2359304 | tf_op jit(solution)/shard_map/ppermute | solution.py:25
  57.2 33.5 %collective-permute-start.3 = (bf16[512,768]{1,0:T(8,128)(2,1)S(1)}, bf16[512,768]{1,0:T(8,128)(2,1)S(1)}, u32[]{:S(2)}, u32[]{:S(2)}) collective-permute-start(bf16[512,768]{1,0:T(8,128)(2,1)S(1)} %collective-permute-done.2.refs_3_), channel_id=1, source_target_pairs={{0,8},{4,12},{8,16},{12,20},{16,24},{20,28},{1,9},{5,13},{9,17},{1... | collective-permute-start | bytes 2359304 | tf_op jit(solution)/shard_map/ppermute | solution.py:25
  63.0 65.7 %collective-permute-start.8 = (bf16[768,768]{1,0:T(8,128)(2,1)}, bf16[768,768]{1,0:T(8,128)(2,1)}, u32[]{:S(2)}, u32[]{:S(2)}) collective-permute-start(bf16[768,768]{1,0:T(8,128)(2,1)} %constant_dynamic-slice_fusion.8), channel_id=1, source_target_pairs={{0,1},{1,0},{2,3},{3,2},{4,5},{5,4},{6,7},{7,6},{8,9},{9,8},{10,11... | collective-permute-start | bytes 3538952 | tf_op jit(solution)/shard_map/ppermute | solution.py:25
  66.2 63.9 %collective-permute-start.13 = (bf16[768,768]{1,0:T(8,128)(2,1)}, bf16[768,768]{1,0:T(8,128)(2,1)}, u32[]{:S(2)}, u32[]{:S(2)}) collective-permute-start(bf16[768,768]{1,0:T(8,128)(2,1)} %get-tuple-element.45), channel_id=1, source_target_pairs={{0,2},{1,3},{2,0},{3,1},{4,6},{5,7},{6,4},{7,5},{8,10},{9,11},{10,... | collective-permute-start | bytes 3538952 | tf_op jit(solution)/shard_map/ppermute | solution.py:25
  70.4 24.3 %collective-permute-start.20 = (bf16[384,640]{1,0:T(8,128)(2,1)}, bf16[384,640]{1,0:T(8,128)(2,1)}, u32[]{:S(2)}, u32[]{:S(2)}) collective-permute-start(bf16[384,640]{1,0:T(8,128)(2,1)} %pad_maximum_fusion), channel_id=1, source_target_pairs={{0,4},{4,0},{8,12},{12,8},{16,20},{20,16},{24,28},{28,24},{1,5},{5... | collective-permute-start | bytes 1474568 | tf_op jit(solution)/shard_map/ppermute | solution.py:25
  91.6 31.3 %collective-permute-start.4 = (bf16[512,768]{1,0:T(8,128)(2,1)}, bf16[512,768]{1,0:T(8,128)(2,1)}, u32[]{:S(2)}, u32[]{:S(2)}) collective-permute-start(bf16[512,768]{1,0:T(8,128)(2,1)} %broadcast_select_fusion), channel_id=1, source_target_pairs={{8,16},{12,20},{16,24},{20,28},{9,17},{13,21},{17,25},{21,29},{10,... | collective-permute-start | bytes 2359304 | tf_op jit(solution)/shard_map/ppermute | solution.py:25
  94.7 50.0 %collective-permute-start.14 = (bf16[768,768]{1,0:T(8,128)(2,1)}, bf16[768,768]{1,0:T(8,128)(2,1)}, u32[]{:S(2)}, u32[]{:S(2)}) collective-permute-start(bf16[768,768]{1,0:T(8,128)(2,1)} %get-tuple-element.44), channel_id=1, source_target_pairs={{0,3},{1,2},{2,1},{3,0},{4,7},{5,6},{6,5},{7,4},{8,11},{9,10},{10,... | collective-permute-start | bytes 3538952 | tf_op jit(solution)/shard_map/ppermute | solution.py:25
  104.3 22.9 %collective-permute-start.21 = (bf16[768,256]{1,0:T(8,128)(2,1)S(1)}, bf16[768,256]{1,0:T(8,128)(2,1)S(1)}, u32[]{:S(2)}, u32[]{:S(2)}) collective-permute-start(bf16[768,256]{1,0:T(8,128)(2,1)S(1)} %maximum_select_fusion.2.refs_8_), channel_id=1, source_target_pairs={{0,8},{4,12},{8,16},{12,20},{16,24},{20,28},{1,9},{5,13},{9,17},{1... | collective-permute-start | bytes 1179656 | tf_op jit(solution)/shard_map/ppermute | solution.py:25
  144.7 21.4 %collective-permute-start.22 = (bf16[768,256]{1,0:T(8,128)(2,1)S(1)}, bf16[768,256]{1,0:T(8,128)(2,1)S(1)}, u32[]{:S(2)}, u32[]{:S(2)}) collective-permute-start(bf16[768,256]{1,0:T(8,128)(2,1)S(1)} %maximum_select_fusion.2.refs_8_), channel_id=1, source_target_pairs={{8,0},{12,4},{16,8},{20,12},{24,16},{28,20},{9,1},{13,5},{17,9},{2... | collective-permute-start | bytes 1179656 | tf_op jit(solution)/shard_map/ppermute | solution.py:25
  146.0 20.6 %collective-permute-start.23 = (bf16[768,256]{1,0:T(8,128)(2,1)S(1)}, bf16[768,256]{1,0:T(8,128)(2,1)S(1)}, u32[]{:S(2)}, u32[]{:S(2)}) collective-permute-start(bf16[768,256]{1,0:T(8,128)(2,1)S(1)} %collective-permute-done.21.refs_9_), channel_id=1, source_target_pairs={{8,16},{12,20},{16,24},{20,28},{9,17},{13,21},{17,25},{21,29},{10,... | collective-permute-start | bytes 1179656 | tf_op jit(solution)/shard_map/ppermute | solution.py:25
  147.9 39.8 %collective-permute-start.35 = (bf16[768,384]{1,0:T(8,128)(2,1)S(1)}, bf16[768,384]{1,0:T(8,128)(2,1)S(1)}, u32[]{:S(2)}, u32[]{:S(2)}) collective-permute-start(bf16[768,384]{1,0:T(8,128)(2,1)S(1)} %maximum_select_fusion.1.refs_2_), channel_id=1, source_target_pairs={{0,8},{4,12},{8,16},{12,20},{16,24},{20,28},{1,9},{5,13},{9,17},{1... | collective-permute-start | bytes 1769480 | tf_op jit(solution)/shard_map/ppermute | solution.py:25
  155.4 30.3 %collective-permute-start.24 = (bf16[768,256]{1,0:T(8,128)(2,1)S(1)}, bf16[768,256]{1,0:T(8,128)(2,1)S(1)}, u32[]{:S(2)}, u32[]{:S(2)}) collective-permute-start(bf16[768,256]{1,0:T(8,128)(2,1)S(1)} %maximum_select_fusion.2.refs_8_), channel_id=1, source_target_pairs={{16,0},{20,4},{24,8},{28,12},{17,1},{21,5},{25,9},{29,13},{18,2},{... | collective-permute-start | bytes 1179656 | tf_op jit(solution)/shard_map/ppermute | solution.py:25
  156.7 29.5 %collective-permute-start.26 = (bf16[768,256]{1,0:T(8,128)(2,1)S(1)}, bf16[768,256]{1,0:T(8,128)(2,1)S(1)}, u32[]{:S(2)}, u32[]{:S(2)}) collective-permute-start(bf16[768,256]{1,0:T(8,128)(2,1)S(1)} %maximum_select_fusion.2.refs_8_), channel_id=1, source_target_pairs={{24,0},{28,4},{25,1},{29,5},{26,2},{30,6},{27,3},{31,7}} | collective-permute-start | bytes 1179656 | tf_op jit(solution)/shard_map/ppermute | solution.py:25
  166.1 22.3 %collective-permute-start.16 = (bf16[256,768]{1,0:T(8,128)(2,1)S(1)}, bf16[256,768]{1,0:T(8,128)(2,1)S(1)}, u32[]{:S(2)}, u32[]{:S(2)}) collective-permute-start(bf16[256,768]{1,0:T(8,128)(2,1)S(1)} %get-tuple-element.30), channel_id=1, source_target_pairs={{0,2},{1,3},{2,0},{3,1},{4,6},{5,7},{6,4},{7,5},{8,10},{9,11},{10,... | collective-permute-start | bytes 1179656 | tf_op jit(solution)/shard_map/ppermute | solution.py:25
  166.7 22.2 %collective-permute-start.25 = (bf16[768,256]{1,0:T(8,128)(2,1)S(1)}, bf16[768,256]{1,0:T(8,128)(2,1)S(1)}, u32[]{:S(2)}, u32[]{:S(2)}) collective-permute-start(bf16[768,256]{1,0:T(8,128)(2,1)S(1)} %collective-permute-done.23.refs_11_), channel_id=1, source_target_pairs={{16,24},{20,28},{17,25},{21,29},{18,26},{22,30},{19,27},{23,31}} | collective-permute-start | bytes 1179656 | tf_op jit(solution)/shard_map/ppermute | solution.py:25
  186.2 19.9 %collective-permute-start.27 = (bf16[256,768]{1,0:T(8,128)(2,1)S(1)}, bf16[256,768]{1,0:T(8,128)(2,1)S(1)}, u32[]{:S(2)}, u32[]{:S(2)}) collective-permute-start(bf16[256,768]{1,0:T(8,128)(2,1)S(1)} %get-tuple-element.30), channel_id=1, source_target_pairs={{0,4},{4,0},{8,12},{12,8},{16,20},{20,16},{24,28},{28,24},{1,5},{5... | collective-permute-start | bytes 1179656 | tf_op jit(solution)/shard_map/ppermute | solution.py:25
  188.3 25.2 %collective-permute-start.29 = (bf16[256,768]{1,0:T(8,128)(2,1)S(1)}, bf16[256,768]{1,0:T(8,128)(2,1)S(1)}, u32[]{:S(2)}, u32[]{:S(2)}) collective-permute-start(bf16[256,768]{1,0:T(8,128)(2,1)S(1)} %collective-permute-done.16.refs_2_), channel_id=1, source_target_pairs={{0,4},{4,0},{8,12},{12,8},{16,20},{20,16},{24,28},{28,24},{1,5},{5... | collective-permute-start | bytes 1179656 | tf_op jit(solution)/shard_map/ppermute | solution.py:25
  188.8 27.4 %collective-permute-start.15 = (bf16[512,768]{1,0:T(8,128)(2,1)}, bf16[512,768]{1,0:T(8,128)(2,1)S(1)}, u32[]{:S(2)}, u32[]{:S(2)}) collective-permute-start(bf16[512,768]{1,0:T(8,128)(2,1)} %get-tuple-element.21.refs_0_.refs_4_), channel_id=1, source_target_pairs={{0,1},{1,0},{2,3},{3,2},{4,5},{5,4},{6,7},{7,6},{8,9},{9,8},{10,11... | collective-permute-start | bytes 2359304 | tf_op jit(solution)/shard_map/ppermute | solution.py:25
  213.5 21.9 %collective-permute-start.36 = (bf16[768,384]{1,0:T(8,128)(2,1)S(1)}, bf16[768,384]{1,0:T(8,128)(2,1)S(1)}, u32[]{:S(2)}, u32[]{:S(2)}) collective-permute-start(bf16[768,384]{1,0:T(8,128)(2,1)S(1)} %maximum_select_fusion.1.refs_2_), channel_id=1, source_target_pairs={{8,0},{12,4},{16,8},{20,12},{24,16},{28,20},{9,1},{13,5},{17,9},{2... | collective-permute-start | bytes 1769480 | tf_op jit(solution)/shard_map/ppermute | solution.py:25
  214.8 21.9 %collective-permute-start.37 = (bf16[768,384]{1,0:T(8,128)(2,1)S(1)}, bf16[768,384]{1,0:T(8,128)(2,1)S(1)}, u32[]{:S(2)}, u32[]{:S(2)}) collective-permute-start(bf16[768,384]{1,0:T(8,128)(2,1)S(1)} %collective-permute-done.35.refs_3_), channel_id=1, source_target_pairs={{8,16},{12,20},{16,24},{20,28},{9,17},{13,21},{17,25},{21,29},{10,... | collective-permute-start | bytes 1769480 | tf_op jit(solution)/shard_map/ppermute | solution.py:25
  235.5 29.6 %collective-permute-start.38 = (bf16[768,384]{1,0:T(8,128)(2,1)S(1)}, bf16[768,384]{1,0:T(8,128)(2,1)S(1)}, u32[]{:S(2)}, u32[]{:S(2)}) collective-permute-start(bf16[768,384]{1,0:T(8,128)(2,1)S(1)} %collective-permute-done.36.refs_4_), channel_id=1, source_target_pairs={{8,0},{12,4},{16,8},{20,12},{9,1},{13,5},{17,9},{21,13},{10,2},{14... | collective-permute-start | bytes 1769480 | tf_op jit(solution)/shard_map/ppermute | solution.py:25
  236.8 28.3 %collective-permute-start.39 = (bf16[768,384]{1,0:T(8,128)(2,1)S(1)}, bf16[768,384]{1,0:T(8,128)(2,1)S(1)}, u32[]{:S(2)}, u32[]{:S(2)}) collective-permute-start(bf16[768,384]{1,0:T(8,128)(2,1)S(1)} %collective-permute-done.37.refs_5_), channel_id=1, source_target_pairs={{16,24},{20,28},{17,25},{21,29},{18,26},{22,30},{19,27},{23,31}} | collective-permute-start | bytes 1769480 | tf_op jit(solution)/shard_map/ppermute | solution.py:25
  240.0 40.2 %collective-permute-start.43 = (bf16[512,256]{1,0:T(8,128)(2,1)S(1)}, bf16[512,256]{1,0:T(8,128)(2,1)S(1)}, u32[]{:S(2)}, u32[]{:S(2)}) collective-permute-start(bf16[512,256]{1,0:T(8,128)(2,1)S(1)} %broadcast_select_fusion.1), channel_id=1, source_target_pairs={{8,16},{12,20},{16,24},{20,28},{9,17},{13,21},{17,25},{21,29},{10,... | collective-permute-start | bytes 786440 | tf_op jit(solution)/shard_map/ppermute | solution.py:25
  (34 other events, 583.0 us)
